TPU v7x, 128 devices: a whole 4x4x4 slice. The times are simulated.
128 devices in a mesh: beta: 64 (over z, y, x), grp: 2 (over core).
Axes of the slice: x: 4, y: 4, z: 4, core: 2. Of those that a mesh axis runs over, the one named last changes fastest.
Arguments:
- samples: float32 [128, 8, 128, 128], P('beta', 'grp'), parts along dimension 1, may hold values from -6 to 6
Outputs:
- coeffs: float32 [128, 2, 8, 64, 64], P('beta', None, 'grp'), parts along dimension 2
- power: float32 [8, 64], P('grp'), parts along dimension 0
There are 2 independent parts, one for each index of `grp`. A program takes and returns all parts, laid end to end along the dimension named above; each array names one. Nothing has to cross between parts.
All inputs are finite; a program needn't handle non-finite values.
Results may differ from a plain program's by a relative error of at most 0.0003.
Values sent between devices are 32-bit elements; how exact they have to be, the bound alone decides.
A program may use at most 64 MiB of HBM per device.

v0:
```python
import jax
import jax.numpy as jnp
from jax import lax
from jax.sharding import PartitionSpec as P

HIGHEST = lax.Precision.HIGHEST


def swapped(value, axis, apart):
    mask = 2**apart
    pairs = [(source, source ^ mask) for source in range(lax.axis_size(axis))]
    return lax.ppermute(value, axis, pairs)


def from_everyone(shard, axis):
    peers = lax.axis_size(axis)
    return lax.all_to_all(
        jnp.broadcast_to(shard[None], (peers, *shard.shape)), axis, 0, 0, tiled=True
    )


def taken_together(shard, axis):
    return from_everyone(shard, axis).sum(axis=0)


def beta_angles(spread):
    grid_size = 2 * spread
    return (2.0 * jnp.arange(grid_size, dtype=jnp.float32) + 1.0) * (jnp.pi / (4.0 * spread))


def quadrature(spread):
    angles = beta_angles(spread)
    odd_terms = 2.0 * jnp.arange(spread, dtype=jnp.float32) + 1.0
    series = jnp.sum(jnp.sin(angles[:, None] * odd_terms[None, :]) / odd_terms[None, :], axis=1)
    return 2.0 / spread * jnp.sin(angles) * series


def gamma_table(spread):
    grid_size = 2 * spread
    positions = jnp.arange(grid_size, dtype=jnp.int32)
    orders = jnp.arange(spread, dtype=jnp.int32)
    phase_index = positions[:, None] * orders[None, :] % grid_size
    angles = phase_index.astype(jnp.float32) * (2.0 * jnp.pi / grid_size)
    return jnp.concatenate([jnp.cos(angles), -jnp.sin(angles)], axis=1)


def alpha_table(spread, row_index):
    grid_size = 2 * spread
    positions = jnp.arange(grid_size, dtype=jnp.int32)
    phase_index = row_index[:, None] * positions[None, :] % grid_size
    angles = phase_index.astype(jnp.float32) * (2.0 * jnp.pi / grid_size)
    cosine = jnp.cos(angles) / grid_size
    sine_part = jnp.sin(angles) / grid_size
    real_rows = jnp.stack([cosine, sine_part], axis=1)
    imag_rows = jnp.stack([-sine_part, cosine], axis=1)
    return jnp.stack([real_rows, imag_rows], axis=0)


def log_factorial(value, float_type):
    return lax.lgamma((value + 1).astype(float_type))


def wigner_start(alpha_order, gamma_order, log_cosine, log_sine):
    float_type = log_cosine.dtype
    lowest = jnp.maximum(jnp.abs(alpha_order), gamma_order)
    shift_low = jnp.maximum(0, gamma_order - alpha_order)
    magnitude = 0.5 * (
        log_factorial(lowest + alpha_order, float_type)
        + log_factorial(lowest - alpha_order, float_type)
        + log_factorial(lowest + gamma_order, float_type)
        + log_factorial(lowest - gamma_order, float_type)
    )
    magnitude = (
        magnitude
        - log_factorial(lowest + gamma_order - shift_low, float_type)
        - log_factorial(shift_low, float_type)
    )
    magnitude = magnitude - log_factorial(alpha_order - gamma_order + shift_low, float_type)
    magnitude = magnitude - log_factorial(lowest - alpha_order - shift_low, float_type)
    cos_power = (2 * lowest + gamma_order - alpha_order - 2 * shift_low).astype(float_type)
    sin_power = (alpha_order - gamma_order + 2 * shift_low).astype(float_type)
    parity = (alpha_order - gamma_order + shift_low) % 2
    sign_factor = (1 - 2 * parity).astype(float_type)
    return sign_factor * jnp.exp(magnitude + cos_power * log_cosine + sin_power * log_sine)


def advance(degree, carried, alpha_order, gamma_order, cos_angles, start_value, lowest):
    former, current = carried
    float_type = current.dtype
    previous = (degree - 1).astype(float_type)
    alpha_float = alpha_order.astype(float_type)
    gamma_float = gamma_order.astype(float_type)
    cross_ratio = alpha_float * gamma_float / jnp.maximum(previous * (previous + 1.0), 1.0)
    upper_term = ((previous + 1.0) * (previous + 1.0) - alpha_float * alpha_float) * (
        (previous + 1.0) * (previous + 1.0) - gamma_float * gamma_float
    )
    lower_term = (previous * previous - alpha_float * alpha_float) * (
        previous * previous - gamma_float * gamma_float
    )
    root_upper = jnp.sqrt(jnp.maximum(upper_term, 1.0))
    forward = (previous + 1.0) * (2.0 * previous + 1.0) / root_upper
    backward = (
        (previous + 1.0)
        * jnp.sqrt(jnp.maximum(lower_term, 0.0))
        / (jnp.maximum(previous, 1.0) * root_upper)
    )
    recurred = forward * (cos_angles - cross_ratio) * current - backward * former
    renewed = jnp.where(degree == lowest, start_value, recurred)
    return (current, renewed)


def degree_rows(row_index, weighted, spread):
    stride = 8
    grid_size = 2 * spread
    group_size = row_index.shape[0]
    channels = weighted.shape[2]
    block_count = spread // stride
    alpha_order = jnp.where(row_index < spread, row_index, row_index - grid_size)[:, None, None]
    gamma_order = jnp.arange(spread, dtype=jnp.int32)[None, None, :]
    angles = beta_angles(spread)
    cos_angles = jnp.cos(angles)[None, :, None]
    log_cosine = jnp.log(jnp.cos(0.5 * angles))[None, :, None]
    log_sine = jnp.log(jnp.sin(0.5 * angles))[None, :, None]
    lowest = jnp.maximum(jnp.abs(alpha_order), gamma_order)
    start_value = wigner_start(alpha_order, gamma_order, log_cosine, log_sine)
    first_block = jnp.min(jnp.abs(alpha_order)) // stride
    empty_state = jnp.zeros((group_size, grid_size, spread), jnp.float32)

    def compute_block(operands):
        block_index, former, current = operands
        levels = []
        for offset in range(stride):
            former, current = advance(
                block_index * stride + offset,
                (former, current),
                alpha_order,
                gamma_order,
                cos_angles,
                start_value,
                lowest,
            )
            levels.append(current)
        stacked = jnp.stack(levels, axis=0)
        block_part = jnp.einsum("jgkq,kgcq->gcjq", stacked, weighted, precision=HIGHEST)
        return (former, current, block_part)

    def skip_block(operands):
        block_index, former, current = operands
        return (former, current, jnp.zeros((group_size, channels, stride, spread), jnp.float32))

    def block_step(carried, block_index):
        former, current = carried
        former, current, block_part = lax.cond(
            block_index >= first_block, compute_block, skip_block, (block_index, former, current)
        )
        return ((former, current), block_part)

    _, parts = lax.scan(
        block_step, (empty_state, empty_state), jnp.arange(block_count, dtype=jnp.int32)
    )
    output = jnp.transpose(parts, (1, 2, 0, 3, 4)).reshape(group_size, channels, spread, spread)
    degree_scale = 8.0 * jnp.sqrt(2.0 * jnp.arange(spread, dtype=jnp.float32) + 1.0)
    return output * degree_scale[None, None, :, None]


def degree_energy(coeffs, functions, spread):
    split_view = coeffs.reshape(coeffs.shape[0], 2, functions, spread, spread)
    multiplicity = jnp.where(jnp.arange(spread) == 0, 1.0, 2.0).astype(jnp.float32)
    energy_sum = jnp.sum(split_view * split_view * multiplicity, axis=(0, 1, 4))
    degrees = 2.0 * jnp.arange(spread, dtype=jnp.float32) + 1.0
    return energy_sum / (degrees * degrees)[None, :]


def local(samples):
    devices = lax.axis_size("beta")
    device = lax.axis_index("beta")
    local_beta = samples.shape[0]
    functions = samples.shape[1]
    grid_size = samples.shape[2]
    spread = grid_size // 2
    channels = 2 * functions
    row_count = grid_size // devices
    natural_rows = jnp.arange(grid_size, dtype=jnp.int32)
    folded = natural_rows.reshape(2, devices // 2, row_count // 2, 2)
    row_order = jnp.stack([folded[:, :, :, 0], folded[::-1, :, :, 1]], axis=3).reshape(grid_size)
    halfway = jnp.einsum("kfag,gx->kfax", samples, gamma_table(spread), precision=HIGHEST)
    halfway = halfway.reshape(local_beta, functions, grid_size, 2, spread)
    spectrum = jnp.einsum(
        "kfacq,spca->kpsfq", halfway, alpha_table(spread, row_order), precision=HIGHEST
    )
    spectrum = spectrum.reshape(local_beta, grid_size, channels, spread)
    received = lax.all_to_all(spectrum, "beta", split_axis=1, concat_axis=0, tiled=True)
    weighted = received * quadrature(spread)[:, None, None, None]
    owned_rows = lax.dynamic_slice_in_dim(row_order, device * row_count, row_count)
    computed = degree_rows(owned_rows, weighted, spread)
    power_part = degree_energy(computed, functions, spread)
    kept = computed[0::2]
    lent = computed[1::2]
    returned = swapped(lent, "beta", devices.bit_length() - 2)
    coeffs = jnp.stack([kept, returned], axis=1).reshape(row_count, channels, spread, spread)
    power = taken_together(power_part, "beta")
    coeffs = coeffs.reshape(row_count, 2, functions, spread, spread)
    return (coeffs, power)


def solution(mesh):
    return jax.shard_map(
        local,
        mesh=mesh,
        in_specs=(P("beta", "grp", None, None),),
        out_specs=(P("beta", None, "grp", None, None), P("grp", None)),
        check_vma=False,
    )
```

profile of v0, /device:TPU:0, one launch (start us, length us, event | category | flops | bytes accessed | tf_op | source)
XLA Modules:
  0.0 99.0 jit_solution(18264558040937235246)
XLA Ops:
  1.1 0.3 sine_multiply_fusion
  1.5 0.2 copy-done
  1.7 0.6 fusion.30
  2.3 0.6 convolution_bitcast_fusion.1
  2.9 0.5 copy.59
  3.5 1.4 %reshape.2616 = f32[64,1,2048]{2,1,0:T(1,128)} reshape(f32[128,2,8,64]{3,2,1,0:T(8,128)S(1)} %bitcast.243) | data formatting | bytes 1048576
  4.9 11.5 %all-to-all-start = ((f32[64,1,2048]{2,1,0:T(1,128)}), f32[64,1,2048]{2,1,0:T(1,128)S(1)}, u32[]{:S(2)}, u32[]{:S(2)}) async-start(f32[64,1,2048]{2,1,0:T(1,128)} %reshape.2616), calls=%async_computation | async-start | bytes 1048576 | tf_op jit(solution)/shard_map/all_to_all | solution.py:192
  16.5 0.7 abs_reduce_fusion
  20.2 0.3 fusion.58
  20.5 9.3 %all-to-all-done = f32[64,1,2048]{2,1,0:T(1,128)S(1)} async-done(((f32[64,1,2048]{2,1,0:T(1,128)}), f32[64,1,2048]{2,1,0:T(1,128)S(1)}, u32[]{:S(2)}, u32[]{:S(2)}) %all-to-all-start) | async-done | bytes 524320 | tf_op jit(solution)/shard_map/all_to_all | solution.py:192
  29.8 0.5 broadcast.2750
  30.3 1.9 %reduce.3 = f32[64,2048]{1,0:T(8,128)S(1)} reduce(f32[64,1,2048]{2,1,0:T(1,128)S(1)} %all-to-all-done, f32[]{:T(128)} %broadcast.2750), dimensions={1}, to_apply=%all_to_all.16.reduce_sub_computation | reduce | bytes 1048580 | tf_op jit(solution)/shard_map/all_to_all | solution.py:192
  32.2 0.4 reshape.2617
  32.9 0.5 copy.62
  33.4 46.3 %while.16 = (s32[]{:T(128)}, f32[2,128,64]{1,2,0:T(8,128)S(1)}, f32[2,128,64]{1,2,0:T(8,128)S(1)}, f32[8,2,8,8,64]{4,3,0,2,1:T(8,128)S(1)}, s32[8]{0:T(128)S(1)}...) while((s32[]{:T(128)}, f32[2,128,64]{1,2,0:T(8,128)S(1)}, ...), condition=%wide.region_5.6_spmd.clone.clone, body=%wide.region_2.5_spmd.clone.clone.sunk | while | flops 13465411 | bytes 3031079 | solution.py:158
  33.5 0.6 dynamic_slice.13
  34.6 4.4 %conditional.4 = (f32[2,128,64]{1,2,0:T(8,128)S(1)}, f32[2,128,64]{1,2,0:T(8,128)S(1)}, f32[1,2,8,8,64]{2,3,4,1,0:T(8,128)S(1)}) conditional(s32[]{:T(128)} %convert_element_type.314, (f32[2,128,64]{1,2,0:T(8,128)S(1)}, f32[2,128,64]{1,2,0:T(8,128)S(1)}) %tuple.142, (s32[]{:T(128)}, s32[2]{0:T(128)S(1)}, s32[2,1,1]{0,2,1:T(1,128)S(1)}, ...), branch_computations={%region_3.3_spmd, %region_4.4_spmd.clone} | conditional | flops 13465407 | bytes 2832748 | solution.py:153
  36.4 0.8 fusion.11
  37.2 0.8 stack.67
  38.0 1.0 convolution_bitcast_fusion
  39.0 0.2 copy.77
  39.2 0.6 dynamic_slice.13
  40.4 4.4 %conditional.4 = (f32[2,128,64]{1,2,0:T(8,128)S(1)}, f32[2,128,64]{1,2,0:T(8,128)S(1)}, f32[1,2,8,8,64]{2,3,4,1,0:T(8,128)S(1)}) conditional(s32[]{:T(128)} %convert_element_type.314, (f32[2,128,64]{1,2,0:T(8,128)S(1)}, f32[2,128,64]{1,2,0:T(8,128)S(1)}) %tuple.142, (s32[]{:T(128)}, s32[2]{0:T(128)S(1)}, s32[2,1,1]{0,2,1:T(1,128)S(1)}, ...), branch_computations={%region_3.3_spmd, %region_4.4_spmd.clone} | conditional | flops 13465407 | bytes 2832748 | solution.py:153
  42.2 0.8 fusion.11
  43.0 0.8 stack.67
  43.8 1.0 convolution_bitcast_fusion
  44.8 0.2 copy.77
  45.0 0.6 dynamic_slice.13
  46.2 4.4 %conditional.4 = (f32[2,128,64]{1,2,0:T(8,128)S(1)}, f32[2,128,64]{1,2,0:T(8,128)S(1)}, f32[1,2,8,8,64]{2,3,4,1,0:T(8,128)S(1)}) conditional(s32[]{:T(128)} %convert_element_type.314, (f32[2,128,64]{1,2,0:T(8,128)S(1)}, f32[2,128,64]{1,2,0:T(8,128)S(1)}) %tuple.142, (s32[]{:T(128)}, s32[2]{0:T(128)S(1)}, s32[2,1,1]{0,2,1:T(1,128)S(1)}, ...), branch_computations={%region_3.3_spmd, %region_4.4_spmd.clone} | conditional | flops 13465407 | bytes 2832748 | solution.py:153
  48.0 0.8 fusion.11
  48.8 0.8 stack.67
  49.6 1.0 convolution_bitcast_fusion
  50.6 0.2 copy.77
  50.8 0.6 dynamic_slice.13
  52.0 4.4 %conditional.4 = (f32[2,128,64]{1,2,0:T(8,128)S(1)}, f32[2,128,64]{1,2,0:T(8,128)S(1)}, f32[1,2,8,8,64]{2,3,4,1,0:T(8,128)S(1)}) conditional(s32[]{:T(128)} %convert_element_type.314, (f32[2,128,64]{1,2,0:T(8,128)S(1)}, f32[2,128,64]{1,2,0:T(8,128)S(1)}) %tuple.142, (s32[]{:T(128)}, s32[2]{0:T(128)S(1)}, s32[2,1,1]{0,2,1:T(1,128)S(1)}, ...), branch_computations={%region_3.3_spmd, %region_4.4_spmd.clone} | conditional | flops 13465407 | bytes 2832748 | solution.py:153
  53.8 0.8 fusion.11
  54.6 0.8 stack.67
  55.4 1.0 convolution_bitcast_fusion
  56.6 0.6 dynamic_slice.13
  57.7 4.4 %conditional.4 = (f32[2,128,64]{1,2,0:T(8,128)S(1)}, f32[2,128,64]{1,2,0:T(8,128)S(1)}, f32[1,2,8,8,64]{2,3,4,1,0:T(8,128)S(1)}) conditional(s32[]{:T(128)} %convert_element_type.314, (f32[2,128,64]{1,2,0:T(8,128)S(1)}, f32[2,128,64]{1,2,0:T(8,128)S(1)}) %tuple.142, (s32[]{:T(128)}, s32[2]{0:T(128)S(1)}, s32[2,1,1]{0,2,1:T(1,128)S(1)}, ...), branch_computations={%region_3.3_spmd, %region_4.4_spmd.clone} | conditional | flops 13465407 | bytes 2832748 | solution.py:153
  59.6 0.8 fusion.11
  60.4 0.8 stack.67
  61.2 1.0 convolution_bitcast_fusion
  62.4 0.6 dynamic_slice.13
  63.5 4.4 %conditional.4 = (f32[2,128,64]{1,2,0:T(8,128)S(1)}, f32[2,128,64]{1,2,0:T(8,128)S(1)}, f32[1,2,8,8,64]{2,3,4,1,0:T(8,128)S(1)}) conditional(s32[]{:T(128)} %convert_element_type.314, (f32[2,128,64]{1,2,0:T(8,128)S(1)}, f32[2,128,64]{1,2,0:T(8,128)S(1)}) %tuple.142, (s32[]{:T(128)}, s32[2]{0:T(128)S(1)}, s32[2,1,1]{0,2,1:T(1,128)S(1)}, ...), branch_computations={%region_3.3_spmd, %region_4.4_spmd.clone} | conditional | flops 13465407 | bytes 2832748 | solution.py:153
  65.4 0.8 fusion.11
  66.2 0.8 stack.67
  67.0 1.0 convolution_bitcast_fusion
  68.2 0.6 dynamic_slice.13
  69.3 4.4 %conditional.4 = (f32[2,128,64]{1,2,0:T(8,128)S(1)}, f32[2,128,64]{1,2,0:T(8,128)S(1)}, f32[1,2,8,8,64]{2,3,4,1,0:T(8,128)S(1)}) conditional(s32[]{:T(128)} %convert_element_type.314, (f32[2,128,64]{1,2,0:T(8,128)S(1)}, f32[2,128,64]{1,2,0:T(8,128)S(1)}) %tuple.142, (s32[]{:T(128)}, s32[2]{0:T(128)S(1)}, s32[2,1,1]{0,2,1:T(1,128)S(1)}, ...), branch_computations={%region_3.3_spmd, %region_4.4_spmd.clone} | conditional | flops 13465407 | bytes 2832748 | solution.py:153
  71.2 0.8 fusion.11
  71.9 0.8 stack.67
  72.8 1.0 convolution_bitcast_fusion
  74.0 0.6 dynamic_slice.13
  75.1 4.4 %conditional.4 = (f32[2,128,64]{1,2,0:T(8,128)S(1)}, f32[2,128,64]{1,2,0:T(8,128)S(1)}, f32[1,2,8,8,64]{2,3,4,1,0:T(8,128)S(1)}) conditional(s32[]{:T(128)} %convert_element_type.314, (f32[2,128,64]{1,2,0:T(8,128)S(1)}, f32[2,128,64]{1,2,0:T(8,128)S(1)}) %tuple.142, (s32[]{:T(128)}, s32[2]{0:T(128)S(1)}, s32[2,1,1]{0,2,1:T(1,128)S(1)}, ...), branch_computations={%region_3.3_spmd, %region_4.4_spmd.clone} | conditional | flops 13465407 | bytes 2832748 | solution.py:153
  77.0 0.8 fusion.11
  77.7 0.8 stack.67
  78.6 1.0 convolution_bitcast_fusion
  80.0 0.7 collective-permute-start
  80.7 0.2 fusion.24
  81.2 15.4 %all_to_all.23 = f32[64,1,256]{2,1,0:T(1,128)S(1)} all-to-all(f32[64,1,256]{2,1,0:T(1,128)S(1)} %reshape.2618), channel_id=1, replica_groups=mesh['beta'=64,'grp'=2] {'beta'}, dimensions={0} | all-to-all | bytes 131072 | tf_op jit(solution)/shard_map/all_to_all | solution.py:17
  96.6 0.8 reduce.4
  97.5 0.7 reduce_sum.38
  98.2 0.8 pad_maximum_fusion
  (257 shorter events, 10.9 us)
Async XLA Ops:
  0.6 1.0 %copy-start = (f32[2,4,128,128]{3,2,1,0:T(8,128)S(1)}, f32[2,4,128,128]{3,2,1,0:T(8,128)}, u32[]{:S(2)}) copy-start(f32[2,4,128,128]{3,2,1,0:T(8,128)} %param.5) | copy-start | bytes 1572868
  4.9 24.9 %all-to-all-start = ((f32[64,1,2048]{2,1,0:T(1,128)}), f32[64,1,2048]{2,1,0:T(1,128)S(1)}, u32[]{:S(2)}, u32[]{:S(2)}) async-start(f32[64,1,2048]{2,1,0:T(1,128)} %reshape.2616), calls=%async_computation | async-start | bytes 1048576 | tf_op jit(solution)/shard_map/all_to_all | solution.py:192
  80.0 18.2 %collective-permute-start = (f32[1,8,64,64]{3,2,1,0:T(8,128)S(1)}, f32[1,8,64,64]{3,2,1,0:T(8,128)S(1)}, u32[]{:S(2)}, u32[]{:S(2)}) collective-permute-start(f32[1,8,64,64]{3,2,1,0:T(8,128)S(1)} %get-tuple-element.575), channel_id=1, source_target_pairs={{0,64},{2,66},{4,68},{6,70},{8,72},{10,74},{12,76},{14,78},{16,80}... | collective-permute-start | bytes 393224 | tf_op jit(solution)/shard_map/ppermute | solution.py:12
where the time goes:
time: 99.5 us; the launch traced here: 99 us
  other arithmetic  20.7 us (21%)
  local copies, waits for them, and re-layouts  17.3 us (17%)
  blocking collectives  15.4 us (15%)
  starting transfers between devices  12.2 us (12%)
  loops' own time  11.7 us (12%)
  waiting for transfers between devices  9.26 us (9%)
  matrix products  8.89 us (9%)
  between operations  3.47 us (3%)
    all_to_all x1, blocking collectives, from_everyone(): lax.all_to_all(jnp.broadcast_to(shard[None], (peers, *shard.shape)), axis...  15.4 us
    all_to_all x1, starting transfers between devices, local(): lax.all_to_all(spectrum, 'beta', split_axis=1, concat_axis=0, tiled=True)  11.5 us
    all_to_all x1, waiting for transfers between devices, local(): lax.all_to_all(spectrum, 'beta', split_axis=1, concat_axis=0, tiled=True)  9.26 us
    dot_general x8, matrix products, compute_block(): jnp.einsum('jgkq,kgcq->gcjq', stacked, weighted, precision=HIGHEST)  7.68 us
    another operation x8, loops' own time, block_step(): lax.cond(block_index >= first_block, compute_block, skip_block, (block_in...  7.04 us
    another operation x8, local copies, waits for them, and re-layouts, compute_block(): stacked = jnp.stack(levels, axis=0)  6.64 us
    select_n x8, other arithmetic, advance(): renewed = jnp.where(degree == lowest, start_value, recurred)  6.16 us
    div x64, other arithmetic, advance(): forward = (previous + 1.0) * (2.0 * previous + 1.0) / root_upper  5.32 us
  transfers between devices with their start and end apart: 2, of which 1 were waited for; matrix products, arithmetic and copies ran while one was open for 4% of the time, Pallas kernels for 0%

commit v1 on v0

v1 whole, which is shorter than its diff:
```python
import math

import jax
import jax.numpy as jnp
import numpy as np
from jax import lax
from jax.experimental import pallas as pl
from jax.experimental.pallas import tpu as pltpu
from jax.sharding import PartitionSpec as P

MESH = pl.DeviceIdType.MESH
F32 = jnp.float32
BF16 = jnp.bfloat16

GRID = 128
SPREAD = 64
FUNCTIONS = 4
CHANNELS = 8
DEVICES = 64
PLANES = 4
PLANE = 16
PLANE_ORDER = (0, 1, 3, 2)


def split_bf16(table):
    high = jnp.asarray(table, F32).astype(BF16)
    low = (jnp.asarray(table, F32) - high.astype(F32)).astype(BF16)
    return high, low


def fourier_tables():
    g = np.arange(GRID)
    q = np.arange(SPREAD)
    gamma = 2.0 * np.pi * ((g[:, None] * q[None, :]) % GRID) / GRID
    cosine, minus_sine = np.cos(gamma), -np.sin(gamma)
    first = np.concatenate([cosine, cosine, minus_sine, minus_sine], axis=1)
    j = np.arange(DEVICES)
    alpha = 2.0 * np.pi * ((2 * j[:, None] * g[None, :]) % GRID) / GRID
    c, s = np.cos(alpha) / GRID, np.sin(alpha) / GRID
    second = np.concatenate(
        [np.concatenate([c, s], axis=1), np.concatenate([-s, c], axis=1)], axis=0
    )
    packed = jnp.concatenate([*split_bf16(first), *split_bf16(second)], axis=0)
    turn = 2.0 * np.pi * g / GRID
    ones = np.ones((GRID, SPREAD))
    twist_cos = np.concatenate([ones, np.cos(turn)[:, None] * ones], axis=1)
    twist_sin = np.concatenate([0.0 * ones, np.sin(turn)[:, None] * ones], axis=1)
    return packed, twist_cos, twist_sin


def beta_tables():
    k = np.arange(GRID)
    angles = np.pi * (2 * k + 1) / 256.0
    odd = 2.0 * np.arange(SPREAD) + 1.0
    weight = (2.0 / SPREAD) * np.sin(angles)
    weight = weight * np.sum(np.sin(angles[:, None] * odd) / odd, axis=1)
    columns = [np.cos(angles), np.log(np.cos(angles / 2)), np.log(np.sin(angles / 2)), weight]
    return [np.repeat(column[:, None], GRID, axis=1) for column in columns]


def order_tables():
    lgamma = np.array([math.lgamma(v + 1.0) for v in range(2 * GRID + 1)])
    n = np.arange(GRID)
    p = np.where(n < SPREAD, n, n - GRID)[:, None]
    q = np.arange(SPREAD)[None, :]
    lowest = np.maximum(np.abs(p), q)
    t = np.maximum(0, q - p)
    magnitude = 0.5 * (
        lgamma[lowest + p] + lgamma[lowest - p] + lgamma[lowest + q] + lgamma[lowest - q]
    )
    magnitude = magnitude - lgamma[lowest + q - t] - lgamma[t]
    magnitude = magnitude - lgamma[p - q + t] - lgamma[lowest - p - t]
    sign = 1.0 - 2.0 * ((p - q + t) % 2)
    cos_power = 2 * lowest + q - p - 2 * t
    sin_power = p - q + 2 * t
    multiplicity = np.where(q == 0, 1.0, 2.0)
    rows = [magnitude, sign, cos_power, sin_power, lowest, p, q, multiplicity]
    rows = [np.broadcast_to(row, (GRID, SPREAD)).reshape(DEVICES, 1, 2 * SPREAD) for row in rows]
    return np.concatenate(rows, axis=1).astype(np.float32)


def row_slice(index):
    return pl.ds(pl.multiple_of(index * 16, 16), 16)


def body(
    samples_hbm,
    packed_hbm,
    real_hbm,
    order_hbm,
    coef_ref,
    power_ref,
    samples,
    packed,
    real,
    order,
    spectrum,
    received,
    wigner,
    total,
    forward_rows,
    cross_rows,
    backward_rows,
    shares,
    load_sem,
    send_sem,
    recv_sem,
    share_send_sem,
    share_recv_sem,
):
    me = lax.axis_index("beta")
    plane = me // PLANE
    within = me % PLANE

    def peer(offset):
        return (me + offset) % DEVICES

    barrier = pltpu.get_barrier_semaphore()

    def greet(offset, _):
        pl.semaphore_signal(
            barrier, 1, device_id={"beta": peer(offset)}, device_id_type=MESH
        )
        return 0

    lax.fori_loop(1, DEVICES, greet, 0)
    loads = [
        pltpu.make_async_copy(samples_hbm, samples, load_sem.at[0]),
        pltpu.make_async_copy(packed_hbm, packed, load_sem.at[1]),
        pltpu.make_async_copy(real_hbm, real, load_sem.at[2]),
        pltpu.make_async_copy(order_hbm.at[me], order, load_sem.at[3]),
    ]
    for load in loads:
        load.start()
    for load in loads:
        load.wait()

    def product(left, right):
        return jnp.dot(left, right, preferred_element_type=F32)

    def transform(k, _):
        values = samples[k].reshape(FUNCTIONS * GRID, GRID)
        high = values.astype(BF16)
        low = (values - high.astype(F32)).astype(BF16)
        gamma_high, gamma_low = packed[0:128, :], packed[128:256, :]
        halfway = product(high, gamma_high) + product(high, gamma_low) + product(low, gamma_high)
        twist_cos, twist_sin = real[0:128, :], real[128:256, :]
        alpha_high, alpha_low = packed[256:384, :], packed[384:512, :]
        for f in range(FUNCTIONS):
            part = halfway[f * GRID : (f + 1) * GRID]
            re, im = part[:, :128], part[:, 128:]
            turned = jnp.concatenate(
                [twist_cos * re + twist_sin * im, twist_cos * im - twist_sin * re], axis=0
            )
            turned_high = turned.astype(BF16)
            turned_low = (turned - turned_high.astype(F32)).astype(BF16)
            rows = (
                product(alpha_high, turned_high)
                + product(alpha_low, turned_high)
                + product(alpha_high, turned_low)
            )
            for s in range(2):
                spectrum[pl.ds(k * CHANNELS + s * FUNCTIONS + f, DEVICES, stride=16), :] = rows[
                    s * DEVICES : (s + 1) * DEVICES
                ]
        return 0

    lax.fori_loop(0, 2, transform, 0)

    pl.semaphore_wait(barrier, DEVICES - 1)

    def exchange(other):
        return pltpu.make_async_remote_copy(
            src_ref=spectrum.at[row_slice(other), :],
            dst_ref=received.at[row_slice(me), :],
            send_sem=send_sem.at[other],
            recv_sem=recv_sem.at[me],
            device_id={"beta": other},
            device_id_type=MESH,
        )

    def arrival(other):
        return pltpu.make_async_remote_copy(
            src_ref=spectrum.at[row_slice(other), :],
            dst_ref=received.at[row_slice(other), :],
            send_sem=send_sem.at[other],
            recv_sem=recv_sem.at[other],
            device_id={"beta": other},
            device_id_type=MESH,
        )

    for step in PLANE_ORDER:

        def send(r, _):
            other = (plane + step) % PLANES * PLANE + (within + r) % PLANE
            exchange(other).start()
            return 0

        lax.fori_loop(1 if step == 0 else 0, PLANE, send, 0)

    received[row_slice(me), :] = spectrum[row_slice(me), :]

    alpha_order, gamma_order = order[5:6, :], order[6:7, :]
    lowest = order[4:5, :]
    degree = lax.broadcasted_iota(jnp.int32, (SPREAD, 128), 0).astype(F32)
    previous = degree - 1.0
    upper = (degree * degree - alpha_order * alpha_order) * (
        degree * degree - gamma_order * gamma_order
    )
    lower = (previous * previous - alpha_order * alpha_order) * (
        previous * previous - gamma_order * gamma_order
    )
    root_upper = jnp.sqrt(jnp.maximum(upper, 1.0))
    forward = degree * (2.0 * previous + 1.0) / root_upper
    cross = alpha_order * gamma_order / jnp.maximum(previous * degree, 1.0)
    backward = (
        degree * jnp.sqrt(jnp.maximum(lower, 0.0)) / (jnp.maximum(previous, 1.0) * root_upper)
    )
    forward_rows[...] = forward
    cross_rows[...] = cross
    backward_rows[...] = backward

    cos_angles = real[256:384, :]
    start_value = (
        real[640:768, :]
        * order[1:2, :]
        * jnp.exp(
            order[0:1, :] + order[2:3, :] * real[384:512, :] + order[3:4, :] * real[512:640, :]
        )
    )
    real[384:512, :] = start_value

    half = GRID // 2
    for block in range(2):

        def advance(level, carried):
            former, current = carried
            f_row = forward_rows[pl.ds(level, 1), :]
            c_row = cross_rows[pl.ds(level, 1), :]
            b_row = backward_rows[pl.ds(level, 1), :]
            starts = lowest == level.astype(F32)
            cosine = real[256 + block * half : 256 + (block + 1) * half, :]
            first = real[384 + block * half : 384 + (block + 1) * half, :]
            recurred = f_row * (cosine - c_row) * current - b_row * former
            renewed = jnp.where(starts, first, recurred)
            wigner[pl.ds(pl.multiple_of(level * GRID + block * half, half), half), :] = renewed
            return current, renewed

        empty = cos_angles[:half] * 0.0
        lax.fori_loop(0, SPREAD, advance, (empty, empty))

    for position, step in enumerate(PLANE_ORDER):
        source = (plane + PLANES - step) % PLANES

        def await_one(r, _):
            arrival(source * PLANE + (within + r) % PLANE).wait_recv()
            return 0

        lax.fori_loop(1 if step == 0 else 0, PLANE, await_one, 0)

        def contract(block, _):
            rows = [pl.ds(pl.multiple_of(block * 64 + t * 8, 8), 8) for t in range(8)]
            if position == 0:
                sums = [jnp.zeros((8, 128), F32) for _ in range(8)]
            else:
                sums = [total[rows[t], :] for t in range(8)]
            for kk in range(32):
                k = source * 32 + kk
                values = received[pl.ds(pl.multiple_of(k * 8, 8), 8), :]
                for t in range(8):
                    factor = wigner[pl.ds((block * 8 + t) * GRID + k, 1), :]
                    sums[t] = sums[t] + values * factor
            for t in range(8):
                total[rows[t], :] = sums[t]
            return 0

        lax.fori_loop(0, 8, contract, 0)

    scale = 8.0 * jnp.sqrt(2.0 * degree + 1.0)
    coeffs = []
    for channel in range(CHANNELS):
        value = total[pl.ds(channel, SPREAD, stride=CHANNELS), :] * scale
        coef_ref[channel] = value
        coeffs.append(value)
    squares = jnp.concatenate(
        [coeffs[f] * coeffs[f] + coeffs[f + 4] * coeffs[f + 4] for f in range(FUNCTIONS)], axis=0
    )
    squares_high = squares.astype(BF16)
    squares_low = (squares - squares_high.astype(F32)).astype(BF16)
    multiplicity = jnp.broadcast_to(order[7:8, :], (16, 128)).astype(BF16)

    def lane_sum(values):
        return lax.dot_general(
            multiplicity, values, (((1,), (1,)), ((), ())), preferred_element_type=F32
        )

    energy = lane_sum(squares_high) + lane_sum(squares_low)
    lane = lax.broadcasted_iota(jnp.int32, (1, 128), 1)
    degrees = 2.0 * (lane % SPREAD).astype(F32) + 1.0
    inverse = 1.0 / (degrees * degrees)
    shares[me, 0:1, :] = energy[0:1, :128] * inverse
    shares[me, 1:2, :] = energy[0:1, 128:] * inverse

    def share(other):
        return pltpu.make_async_remote_copy(
            src_ref=shares.at[me],
            dst_ref=shares.at[me],
            send_sem=share_send_sem.at[other],
            recv_sem=share_recv_sem.at[me],
            device_id={"beta": other},
            device_id_type=MESH,
        )

    def share_arrival(other):
        return pltpu.make_async_remote_copy(
            src_ref=shares.at[other],
            dst_ref=shares.at[other],
            send_sem=share_send_sem.at[other],
            recv_sem=share_recv_sem.at[other],
            device_id={"beta": other},
            device_id_type=MESH,
        )

    def send_share(offset, _):
        share(peer(offset)).start()
        return 0

    def await_share(offset, _):
        share_arrival(peer(offset)).wait_recv()
        return 0

    def await_sent(offset, _):
        exchange(peer(offset)).wait_send()
        share(peer(offset)).wait_send()
        return 0

    lax.fori_loop(1, DEVICES, send_share, 0)
    lax.fori_loop(1, DEVICES, await_share, 0)

    result = shares[0]
    for index in range(1, DEVICES):
        result = result + shares[index]
    for f in range(FUNCTIONS):
        power_ref[f : f + 1, :] = result[f // 2 : f // 2 + 1, f % 2 * 64 : f % 2 * 64 + 64]
    lax.fori_loop(1, DEVICES, await_sent, 0)


def local(samples):
    packed, twist_cos, twist_sin = fourier_tables()
    real = jnp.asarray(np.concatenate([twist_cos, twist_sin, *beta_tables()], axis=0), F32)
    order = jnp.asarray(order_tables(), F32)
    hbm = pl.BlockSpec(memory_space=pl.ANY)
    vmem = pl.BlockSpec(memory_space=pltpu.VMEM)
    coef, power = pl.pallas_call(
        body,
        out_shape=(
            jax.ShapeDtypeStruct((CHANNELS, SPREAD, 128), F32),
            jax.ShapeDtypeStruct((FUNCTIONS, SPREAD), F32),
        ),
        in_specs=[hbm] * 4,
        out_specs=(vmem, vmem),
        scratch_shapes=[
            pltpu.VMEM((2, FUNCTIONS, GRID, GRID), F32),
            pltpu.VMEM((512, 256), BF16),
            pltpu.VMEM((768, 128), F32),
            pltpu.VMEM((8, 128), F32),
            pltpu.VMEM((DEVICES * 16, 128), F32),
            pltpu.VMEM((DEVICES * 16, 128), F32),
            pltpu.VMEM((SPREAD * GRID, 128), F32),
            pltpu.VMEM((SPREAD * CHANNELS, 128), F32),
            pltpu.VMEM((SPREAD, 128), F32),
            pltpu.VMEM((SPREAD, 128), F32),
            pltpu.VMEM((SPREAD, 128), F32),
            pltpu.VMEM((DEVICES, 2, 128), F32),
            pltpu.SemaphoreType.DMA((4,)),
            pltpu.SemaphoreType.DMA((DEVICES,)),
            pltpu.SemaphoreType.DMA((DEVICES,)),
            pltpu.SemaphoreType.DMA((DEVICES,)),
            pltpu.SemaphoreType.DMA((DEVICES,)),
        ],
        compiler_params=pltpu.CompilerParams(collective_id=0, has_side_effects=True),
        name="rotation_transform",
    )(samples, packed, real, order)
    coeffs = jnp.stack([coef[:, :, :SPREAD], coef[:, :, SPREAD:]], axis=0)
    return coeffs.reshape(2, 2, FUNCTIONS, SPREAD, SPREAD), power


def solution(mesh):
    return jax.shard_map(
        local,
        mesh=mesh,
        in_specs=(P("beta", "grp", None, None),),
        out_specs=(P("beta", None, "grp", None, None), P("grp", None)),
        check_vma=False,
    )
```

time: 99.5 us -> 34 us (0.34)
  Pallas kernels: 0 us -> 30.6 us
  other arithmetic: 20.7 us -> 0.84 us
  local copies, waits for them, and re-layouts: 17.3 us -> 1.74 us
  blocking collectives: 15.4 us -> 0 us
  starting transfers between devices: 12.2 us -> 0 us
  loops' own time: 11.7 us -> 0 us
  waiting for transfers between devices: 9.26 us -> 0 us
  matrix products: 8.89 us -> 0 us
  between operations: 3.47 us -> 0.65 us
    pallas_call x0 -> x1, Pallas kernels: none -> 30.6 us  [local(): pl.pallas_call(body, out_shape=(jax.ShapeDtypeStruct((CHANNELS, SPREAD, 1...]
    all_to_all x1 -> x0, blocking collectives: 15.4 us -> none  [from_everyone(): lax.all_to_all(jnp.broadcast_to(shard[None], (peers, *shard.shape)), axis...]
    another operation x9 -> x0, loops' own time: 11.7 us -> none  [the longest x8 7.04 us: block_step(): lax.cond(block_index >= first_block, compute_block, skip_block, (block_in...]
    all_to_all x1 -> x0, starting transfers between devices: 11.5 us -> none  [local(): lax.all_to_all(spectrum, 'beta', split_axis=1, concat_axis=0, tiled=True)]
    all_to_all x1 -> x0, waiting for transfers between devices: 9.26 us -> none  [local(): lax.all_to_all(spectrum, 'beta', split_axis=1, concat_axis=0, tiled=True)]
    dot_general x10 -> x0, matrix products: 8.89 us -> none  [the longest x8 7.68 us: compute_block(): jnp.einsum('jgkq,kgcq->gcjq', stacked, weighted, precision=HIGHEST)]
    another operation x9 -> x0, local copies, waits for them, and re-layouts: 6.73 us -> none  [the longest x8 6.64 us: compute_block(): stacked = jnp.stack(levels, axis=0)]
    div x74 -> x0, other arithmetic: 6.29 us -> none  [the longest x64 5.32 us: advance(): forward = (previous + 1.0) * (2.0 * previous + 1.0) / root_upper]
  transfers between devices with their start and end apart: 2 -> 0, of which waited for: 1 -> 0; matrix products, arithmetic and copies ran while one was open for 4% -> 0% of each run, Pallas kernels for 0% -> 0%
where the time goes in v1:
time: 34 us; the launch traced here: 33.8 us
  Pallas kernels  30.6 us (90%)
  local copies, waits for them, and re-layouts  1.74 us (5%)
  other arithmetic  0.84 us (2%)
  between operations  0.65 us (2%)
    pallas_call x1, Pallas kernels, local(): pl.pallas_call(body, out_shape=(jax.ShapeDtypeStruct((CHANNELS, SPREAD, 1...  30.6 us
    slice x1, local copies, waits for them, and re-layouts, local(): coeffs = jnp.stack([coef[:, :, :SPREAD], coef[:, :, SPREAD:]], axis=0)  1.16 us
    another operation x1, other arithmetic, local(): coeffs = jnp.stack([coef[:, :, :SPREAD], coef[:, :, SPREAD:]], axis=0)  0.84 us

profile of v1, /device:TPU:0, one launch (start us, length us, event | category | flops | bytes accessed | tf_op | source)
XLA Modules:
  0.0 33.8 jit_solution(2811686802900425037)
XLA Ops:
  0.6 30.6 %rotation_transform.1 = (f32[8,64,128]{2,1,0:T(8,128)}, f32[4,64]{1,0:T(4,128)}) custom-call(f32[2,4,128,128]{3,2,1,0:T(8,128)} %samples_hbm.1, bf16[512,256]{1,0:T(8,128)(2,1)} %constant.21.packed_hbm, f32[768,128]{1,0:T(8,128)} %constant.10.clone.real_hbm, f32[64,8,128]{2,1,0:T(8,128)} %constant.11.clone.order_hbm), custom_call_target="tpu_custom_call" | custom-call | tf_op jit(solution)/shard_map/rotation_transform/pallas_call | solution.py:354
  31.2 1.2 %fusion = (f32[8,64,64]{2,1,0:T(8,128)S(1)}, f32[8,64,64]{2,1,0:T(8,128)S(1)}) fusion(f32[8,64,128]{2,1,0:T(8,128)} %get-tuple-element.4), kind=kLoop, calls=%fused_computation.1 | loop fusion | bytes 524288 | tf_op jit(solution)/shard_map/slice | solution.py:384
  32.4 0.0 copy-start
  32.4 0.8 %pad_maximum_fusion = f32[2,2,4,64,64]{4,3,2,1,0:T(8,128)} fusion(f32[1,2,4,64,64]{4,3,2,1,0:T(8,128)S(1)} %bitcast.3, f32[1,2,4,64,64]{4,3,2,1,0:T(8,128)S(1)} %bitcast.2), kind=kLoop, calls=%fused_computation | loop fusion | flops 65536 | bytes 524288 | tf_op jit(solution)/shard_map/stack | solution.py:384
  33.3 0.0 copy-done
  33.3 0.6 %copy.10 = f32[4,64]{1,0:T(4,128)} copy(f32[4,64]{1,0:T(4,128)S(1)} %copy-done) | data formatting | bytes 2048
Async XLA Ops:
  32.4 0.8 %copy-start = (f32[4,64]{1,0:T(4,128)S(1)}, f32[4,64]{1,0:T(4,128)}, u32[]{:S(2)}) copy-start(f32[4,64]{1,0:T(4,128)} %get-tuple-element.11) | copy-start | bytes 3076

commit v2 on v1

v2 whole, which is shorter than its diff:
```python
import itertools
import math

import jax
import jax.numpy as jnp
import numpy as np
from jax import lax
from jax.experimental import pallas as pl
from jax.experimental.pallas import tpu as pltpu
from jax.sharding import PartitionSpec as P

MESH = pl.DeviceIdType.MESH
F32 = jnp.float32
BF16 = jnp.bfloat16

GRID = 128
SPREAD = 64
FUNCTIONS = 4
CHANNELS = 8
DEVICES = 64
PLANES = 4
PLANE = 16
RING_HOPS = (0, 1, 2, 1)


def hops(offset):
    return sum(RING_HOPS[step] for step in offset)


def far_first():
    near = sorted(
        (o for o in itertools.product(range(4), repeat=3) if o != (0, 0, 0)), key=hops
    )
    order = []
    for z, y, x in near:
        for turn in ((z, y, x), (y, x, z), (x, z, y)):
            for offset in (turn, tuple((4 - step) % 4 for step in turn)):
                if offset not in order:
                    order.append(offset)
    return order[::-1]


OFFSETS = far_first()
GROUPS = [
    [o for o in OFFSETS if hops(o) >= 4],
    [o for o in OFFSETS if hops(o) == 3],
    [o for o in OFFSETS if hops(o) == 2],
    [o for o in OFFSETS if hops(o) == 1],
]


def split_bf16(table):
    high = jnp.asarray(table, F32).astype(BF16)
    low = (jnp.asarray(table, F32) - high.astype(F32)).astype(BF16)
    return high, low


def fourier_tables():
    g = np.arange(GRID)
    q = np.arange(SPREAD)
    gamma = 2.0 * np.pi * ((g[:, None] * q[None, :]) % GRID) / GRID
    cosine, minus_sine = np.cos(gamma), -np.sin(gamma)
    first = np.concatenate([cosine, cosine, minus_sine, minus_sine], axis=1)
    j = np.arange(DEVICES)
    alpha = 2.0 * np.pi * ((2 * j[:, None] * g[None, :]) % GRID) / GRID
    c, s = np.cos(alpha) / GRID, np.sin(alpha) / GRID
    second = np.concatenate(
        [np.concatenate([c, s], axis=1), np.concatenate([-s, c], axis=1)], axis=0
    )
    packed = jnp.concatenate([*split_bf16(first), *split_bf16(second)], axis=0)
    turn = 2.0 * np.pi * g / GRID
    ones = np.ones((GRID, SPREAD))
    twist_cos = np.concatenate([ones, np.cos(turn)[:, None] * ones], axis=1)
    twist_sin = np.concatenate([0.0 * ones, np.sin(turn)[:, None] * ones], axis=1)
    return packed, twist_cos, twist_sin


def beta_tables():
    k = np.arange(GRID)
    angles = np.pi * (2 * k + 1) / 256.0
    odd = 2.0 * np.arange(SPREAD) + 1.0
    weight = (2.0 / SPREAD) * np.sin(angles)
    weight = weight * np.sum(np.sin(angles[:, None] * odd) / odd, axis=1)
    columns = [np.cos(angles), np.log(np.cos(angles / 2)), np.log(np.sin(angles / 2)), weight]
    return [np.repeat(column[:, None], GRID, axis=1) for column in columns]


def order_tables():
    lgamma = np.array([math.lgamma(v + 1.0) for v in range(2 * GRID + 1)])
    n = np.arange(GRID)
    p = np.where(n < SPREAD, n, n - GRID)[:, None]
    q = np.arange(SPREAD)[None, :]
    lowest = np.maximum(np.abs(p), q)
    t = np.maximum(0, q - p)
    magnitude = 0.5 * (
        lgamma[lowest + p] + lgamma[lowest - p] + lgamma[lowest + q] + lgamma[lowest - q]
    )
    magnitude = magnitude - lgamma[lowest + q - t] - lgamma[t]
    magnitude = magnitude - lgamma[p - q + t] - lgamma[lowest - p - t]
    sign = 1.0 - 2.0 * ((p - q + t) % 2)
    cos_power = 2 * lowest + q - p - 2 * t
    sin_power = p - q + 2 * t
    multiplicity = np.where(q == 0, 1.0, 2.0)
    rows = [magnitude, sign, cos_power, sin_power, lowest, p, q, multiplicity]
    rows = [np.broadcast_to(row, (GRID, SPREAD)).reshape(DEVICES, 1, 2 * SPREAD) for row in rows]
    return np.concatenate(rows, axis=1).astype(np.float32)


def row_slice(index):
    return pl.ds(pl.multiple_of(index * 16, 16), 16)


def body(
    samples_hbm,
    packed_hbm,
    real_hbm,
    order_hbm,
    coef_ref,
    power_ref,
    samples,
    packed,
    real,
    order,
    spectrum,
    received,
    wigner,
    total,
    forward_rows,
    cross_rows,
    backward_rows,
    shares,
    load_sem,
    send_sem,
    recv_sem,
):
    me = lax.axis_index("beta")
    place = (me // 16, me // 4 % 4, me % 4)

    def target(offset):
        z, y, x = ((place[axis] + offset[axis]) % 4 for axis in range(3))
        return z * 16 + y * 4 + x

    def origin(offset):
        return target(tuple((4 - step) % 4 for step in offset))

    loads = [
        pltpu.make_async_copy(samples_hbm, samples, load_sem.at[0]),
        pltpu.make_async_copy(packed_hbm, packed, load_sem.at[1]),
        pltpu.make_async_copy(real_hbm, real, load_sem.at[2]),
        pltpu.make_async_copy(order_hbm.at[me], order, load_sem.at[3]),
    ]
    for load in loads:
        load.start()

    barrier = pltpu.get_barrier_semaphore()
    with jax.named_scope("greet"):
        for offset in OFFSETS:
            pl.semaphore_signal(
                barrier, 1, device_id={"beta": target(offset)}, device_id_type=MESH
            )

    with jax.named_scope("load"):
        for load in loads:
            load.wait()

    def product(left, right):
        return jnp.dot(left, right, preferred_element_type=F32)

    def transform(k, _):
        values = samples[k].reshape(FUNCTIONS * GRID, GRID)
        high = values.astype(BF16)
        low = (values - high.astype(F32)).astype(BF16)
        gamma_high, gamma_low = packed[0:128, :], packed[128:256, :]
        halfway = product(high, gamma_high) + product(high, gamma_low) + product(low, gamma_high)
        twist_cos, twist_sin = real[0:128, :], real[128:256, :]
        alpha_high, alpha_low = packed[256:384, :], packed[384:512, :]
        for f in range(FUNCTIONS):
            part = halfway[f * GRID : (f + 1) * GRID]
            re, im = part[:, :128], part[:, 128:]
            turned = jnp.concatenate(
                [twist_cos * re + twist_sin * im, twist_cos * im - twist_sin * re], axis=0
            )
            turned_high = turned.astype(BF16)
            turned_low = (turned - turned_high.astype(F32)).astype(BF16)
            rows = (
                product(alpha_high, turned_high)
                + product(alpha_low, turned_high)
                + product(alpha_high, turned_low)
            )
            for s in range(2):
                spectrum[pl.ds(k * CHANNELS + s * FUNCTIONS + f, DEVICES, stride=16), :] = rows[
                    s * DEVICES : (s + 1) * DEVICES
                ]
        return 0

    with jax.named_scope("dft"):
        lax.fori_loop(0, 2, transform, 0)

    with jax.named_scope("barrier_wait"):
        pl.semaphore_wait(barrier, DEVICES - 1)

    with jax.named_scope("send"):
        for group, members in enumerate(GROUPS):
            for offset in members:
                other = target(offset)
                pltpu.make_async_remote_copy(
                    src_ref=spectrum.at[row_slice(other), :],
                    dst_ref=received.at[row_slice(me), :],
                    send_sem=send_sem.at[0],
                    recv_sem=recv_sem.at[group],
                    device_id={"beta": other},
                    device_id_type=MESH,
                ).start()

    def await_group(group):
        count = len(GROUPS[group])
        pltpu.make_async_remote_copy(
            src_ref=spectrum.at[0 : count * 16, :],
            dst_ref=received.at[0 : count * 16, :],
            send_sem=send_sem.at[0],
            recv_sem=recv_sem.at[group],
            device_id={"beta": target(OFFSETS[0])},
            device_id_type=MESH,
        ).wait_recv()

    received[row_slice(me), :] = spectrum[row_slice(me), :]

    with jax.named_scope("coeff"):
        alpha_order, gamma_order = order[5:6, :], order[6:7, :]
        lowest = order[4:5, :]
        degree = lax.broadcasted_iota(jnp.int32, (SPREAD, 128), 0).astype(F32)
        previous = degree - 1.0
        upper = (degree * degree - alpha_order * alpha_order) * (
            degree * degree - gamma_order * gamma_order
        )
        lower = (previous * previous - alpha_order * alpha_order) * (
            previous * previous - gamma_order * gamma_order
        )
        root_upper = jnp.sqrt(jnp.maximum(upper, 1.0))
        forward = degree * (2.0 * previous + 1.0) / root_upper
        cross = alpha_order * gamma_order / jnp.maximum(previous * degree, 1.0)
        backward = (
            degree * jnp.sqrt(jnp.maximum(lower, 0.0)) / (jnp.maximum(previous, 1.0) * root_upper)
        )
        forward_rows[...] = forward
        cross_rows[...] = cross
        backward_rows[...] = backward

        cos_angles = real[256:384, :]
        start_value = (
            real[640:768, :]
            * order[1:2, :]
            * jnp.exp(
                order[0:1, :] + order[2:3, :] * real[384:512, :] + order[3:4, :] * real[512:640, :]
            )
        )
        real[384:512, :] = start_value

    half = GRID // 2
    with jax.named_scope("wigner"):
        for block in range(2):

            def advance(level, carried):
                former, current = carried
                f_row = forward_rows[pl.ds(level, 1), :]
                c_row = cross_rows[pl.ds(level, 1), :]
                b_row = backward_rows[pl.ds(level, 1), :]
                starts = lowest == level.astype(F32)
                cosine = real[256 + block * half : 256 + (block + 1) * half, :]
                first = real[384 + block * half : 384 + (block + 1) * half, :]
                recurred = f_row * (cosine - c_row) * current - b_row * former
                renewed = jnp.where(starts, first, recurred)
                wigner[pl.ds(pl.multiple_of(level * GRID + block * half, half), half), :] = renewed
                return current, renewed

            empty = cos_angles[:half] * 0.0
            lax.fori_loop(0, SPREAD, advance, (empty, empty))

    for group, members in enumerate(GROUPS):
        with jax.named_scope(f"wait{group}"):
            await_group(group)
        sources = [origin(offset) for offset in members]
        if group == 0:
            sources = [me] + sources

        def contract(block, _):
            rows = [pl.ds(pl.multiple_of(block * 64 + t * 8, 8), 8) for t in range(8)]
            if group == 0:
                sums = [jnp.zeros((8, 128), F32) for _ in range(8)]
            else:
                sums = [total[rows[t], :] for t in range(8)]
            for source in sources:
                for kk in range(2):
                    k = source * 2 + kk
                    values = received[pl.ds(pl.multiple_of(k * 8, 8), 8), :]
                    for t in range(8):
                        factor = wigner[pl.ds((block * 8 + t) * GRID + k, 8, stride=0), :]
                        sums[t] = sums[t] + values * factor
            for t in range(8):
                total[rows[t], :] = sums[t]
            return 0

        with jax.named_scope(f"contract{group}"):
            lax.fori_loop(0, 8, contract, 0)

    with jax.named_scope("finish"):
        scale = 8.0 * jnp.sqrt(2.0 * degree + 1.0)
        coeffs = []
        for channel in range(CHANNELS):
            value = total[pl.ds(channel, SPREAD, stride=CHANNELS), :] * scale
            coeffs.append(value)
        squares = jnp.concatenate(
            [coeffs[f] * coeffs[f] + coeffs[f + 4] * coeffs[f + 4] for f in range(FUNCTIONS)], axis=0
        )
        squares_high = squares.astype(BF16)
        squares_low = (squares - squares_high.astype(F32)).astype(BF16)
        multiplicity = jnp.broadcast_to(order[7:8, :], (16, 128)).astype(BF16)

        def lane_sum(values):
            return lax.dot_general(
                multiplicity, values, (((1,), (1,)), ((), ())), preferred_element_type=F32
            )

        energy = lane_sum(squares_high) + lane_sum(squares_low)
        lane = lax.broadcasted_iota(jnp.int32, (1, 128), 1)
        degrees = 2.0 * (lane % SPREAD).astype(F32) + 1.0
        inverse = 1.0 / (degrees * degrees)
        shares[me, 0:1, :] = energy[0:1, :128] * inverse
        shares[me, 1:2, :] = energy[0:1, 128:] * inverse

    with jax.named_scope("share_send"):
        for offset in OFFSETS:
            pltpu.make_async_remote_copy(
                src_ref=shares.at[me],
                dst_ref=shares.at[me],
                send_sem=send_sem.at[1],
                recv_sem=recv_sem.at[len(GROUPS)],
                device_id={"beta": target(offset)},
                device_id_type=MESH,
            ).start()

    with jax.named_scope("store"):
        for channel in range(CHANNELS):
            coef_ref[0, channel] = coeffs[channel][:, :SPREAD]
            coef_ref[1, channel] = coeffs[channel][:, SPREAD:]

    others = DEVICES - 1
    with jax.named_scope("sent"):
        pltpu.make_async_remote_copy(
            src_ref=spectrum.at[0 : others * 16, :],
            dst_ref=received.at[0 : others * 16, :],
            send_sem=send_sem.at[0],
            recv_sem=recv_sem.at[0],
            device_id={"beta": target(OFFSETS[0])},
            device_id_type=MESH,
        ).wait_send()

    with jax.named_scope("share_wait"):
        shared = pltpu.make_async_remote_copy(
            src_ref=shares.at[0:others],
            dst_ref=shares.at[0:others],
            send_sem=send_sem.at[1],
            recv_sem=recv_sem.at[len(GROUPS)],
            device_id={"beta": target(OFFSETS[0])},
            device_id_type=MESH,
        )
        shared.wait_send()
        shared.wait_recv()

    with jax.named_scope("share_sum"):
        result = shares[0]
        for index in range(1, DEVICES):
            result = result + shares[index]
        for f in range(FUNCTIONS):
            power_ref[f : f + 1, :] = result[f // 2 : f // 2 + 1, f % 2 * 64 : f % 2 * 64 + 64]


def local(samples):
    packed, twist_cos, twist_sin = fourier_tables()
    real = jnp.asarray(np.concatenate([twist_cos, twist_sin, *beta_tables()], axis=0), F32)
    order = jnp.asarray(order_tables(), F32)
    hbm = pl.BlockSpec(memory_space=pl.ANY)
    vmem = pl.BlockSpec(memory_space=pltpu.VMEM)
    coef, power = pl.pallas_call(
        body,
        out_shape=(
            pltpu.VMEM((2, CHANNELS, SPREAD, SPREAD), F32),
            pltpu.VMEM((FUNCTIONS, SPREAD), F32),
        ),
        in_specs=[hbm] * 4,
        out_specs=(vmem, vmem),
        scratch_shapes=[
            pltpu.VMEM((2, FUNCTIONS, GRID, GRID), F32),
            pltpu.VMEM((512, 256), BF16),
            pltpu.VMEM((768, 128), F32),
            pltpu.VMEM((8, 128), F32),
            pltpu.VMEM((DEVICES * 16, 128), F32),
            pltpu.VMEM((DEVICES * 16, 128), F32),
            pltpu.VMEM((SPREAD * GRID, 128), F32),
            pltpu.VMEM((SPREAD * CHANNELS, 128), F32),
            pltpu.VMEM((SPREAD, 128), F32),
            pltpu.VMEM((SPREAD, 128), F32),
            pltpu.VMEM((SPREAD, 128), F32),
            pltpu.VMEM((DEVICES, 2, 128), F32),
            pltpu.SemaphoreType.DMA((4,)),
            pltpu.SemaphoreType.DMA((2,)),
            pltpu.SemaphoreType.DMA((len(GROUPS) + 1,)),
        ],
        compiler_params=pltpu.CompilerParams(collective_id=0, has_side_effects=True),
        name="rotation_transform",
    )(samples, packed, real, order)
    return coef.reshape(2, 2, FUNCTIONS, SPREAD, SPREAD), power


def solution(mesh):
    return jax.shard_map(
        local,
        mesh=mesh,
        in_specs=(P("beta", "grp", None, None),),
        out_specs=(P("beta", None, "grp", None, None), P("grp", None)),
        check_vma=False,
    )
```

time: 34 us -> 29 us (0.85)
  Pallas kernels: 30.6 us -> 26.9 us
  other arithmetic: 0.84 us -> 0 us
  local copies, waits for them, and re-layouts: 1.74 us -> 1.37 us
    pallas_call x1, Pallas kernels: 30.6 us -> 26.9 us  [local(): pl.pallas_call(body, out_shape=(pltpu.VMEM((2, CHANNELS, SPREAD, SPREAD),...]
    slice x1 -> x0, local copies, waits for them, and re-layouts: 1.16 us -> none  [local(): coeffs = jnp.stack([coef[:, :, :SPREAD], coef[:, :, SPREAD:]], axis=0)]
    another operation x1 -> x0, other arithmetic: 0.84 us -> none  [local(): coeffs = jnp.stack([coef[:, :, :SPREAD], coef[:, :, SPREAD:]], axis=0)]
    unnamed x3 -> x2, local copies, waits for them, and re-layouts: 0.58 us -> 1.37 us
where the time goes in v2:
time: 29 us; the launch traced here: 28.9 us
  Pallas kernels  26.9 us (93%)
  local copies, waits for them, and re-layouts  1.37 us (5%)
  between operations  0.64 us (2%)
    pallas_call x1, Pallas kernels, local(): pl.pallas_call(body, out_shape=(pltpu.VMEM((2, CHANNELS, SPREAD, SPREAD),...  26.9 us
    unnamed x2, local copies, waits for them, and re-layouts  1.37 us

profile of v2, /device:TPU:0, one launch (start us, length us, event | category | flops | bytes accessed | tf_op | source)
XLA Modules:
  0.0 28.9 jit_solution(10662456632719639546)
XLA Ops:
  0.6 26.9 %rotation_transform.1 = (f32[2,8,64,64]{3,2,1,0:T(8,128)S(1)}, f32[4,64]{1,0:T(4,128)S(1)}) custom-call(f32[2,4,128,128]{3,2,1,0:T(8,128)} %samples_hbm.1, bf16[512,256]{1,0:T(8,128)(2,1)} %constant.21.packed_hbm, f32[768,128]{1,0:T(8,128)} %constant.10.clone.real_hbm, f32[64,8,128]{2,1,0:T(8,128)} %constant.11.clone.order_hbm), custom_call_target="tpu_custom_call" | custom-call | tf_op jit(solution)/shard_map/rotation_transform/pallas_call | solution.py:384
  27.5 0.8 %copy.11 = f32[2,2,4,64,64]{4,3,2,1,0:T(8,128)} copy(f32[2,2,4,64,64]{4,3,2,1,0:T(8,128)S(1)} %bitcast.1) | data formatting | bytes 524288
  28.3 0.6 %copy.12 = f32[4,64]{1,0:T(4,128)} copy(f32[4,64]{1,0:T(4,128)S(1)} %get-tuple-element.7) | data formatting | bytes 2048

commit v3 on v2

v3 whole, which is shorter than its diff:
```python
import itertools
import math

import jax
import jax.numpy as jnp
import numpy as np
from jax import lax
from jax.experimental import pallas as pl
from jax.experimental.pallas import tpu as pltpu
from jax.sharding import PartitionSpec as P

MESH = pl.DeviceIdType.MESH
F32 = jnp.float32
BF16 = jnp.bfloat16

GRID = 128
SPREAD = 64
FUNCTIONS = 4
CHANNELS = 8
DEVICES = 64
OTHERS = DEVICES - 1
HALF = DEVICES * CHANNELS
RING_HOPS = (0, 1, 2, 1)


def hops(offset):
    return sum(RING_HOPS[step] for step in offset)


def far_first():
    near = sorted(
        (o for o in itertools.product(range(4), repeat=3) if o != (0, 0, 0)), key=hops
    )
    order = []
    for z, y, x in near:
        for turn in ((z, y, x), (y, x, z), (x, z, y)):
            for offset in (turn, tuple((4 - step) % 4 for step in turn)):
                if offset not in order:
                    order.append(offset)
    return order[::-1]


OFFSETS = far_first()


def split_bf16(table):
    high = jnp.asarray(table, F32).astype(BF16)
    low = (jnp.asarray(table, F32) - high.astype(F32)).astype(BF16)
    return high, low


def fourier_tables():
    g = np.arange(GRID)
    q = np.arange(SPREAD)
    gamma = 2.0 * np.pi * ((g[:, None] * q[None, :]) % GRID) / GRID
    cosine, minus_sine = np.cos(gamma), -np.sin(gamma)
    first = np.concatenate([cosine, cosine, minus_sine, minus_sine], axis=1)
    j = np.arange(DEVICES)
    alpha = 2.0 * np.pi * ((2 * j[:, None] * g[None, :]) % GRID) / GRID
    c, s = np.cos(alpha) / GRID, np.sin(alpha) / GRID
    second = np.concatenate(
        [np.concatenate([c, s], axis=1), np.concatenate([-s, c], axis=1)], axis=0
    )
    first_high, first_low = split_bf16(first)
    packed = jnp.concatenate([first_high, first_high, first_low, *split_bf16(second)], axis=0)
    turn = 2.0 * np.pi * g / GRID
    ones = np.ones((GRID, SPREAD))
    twist_cos = np.concatenate([ones, np.cos(turn)[:, None] * ones], axis=1)
    twist_sin = np.concatenate([0.0 * ones, np.sin(turn)[:, None] * ones], axis=1)
    return packed, jnp.asarray(np.concatenate([twist_cos, twist_sin], axis=0), F32)


def beta_tables():
    k = np.arange(GRID).reshape(DEVICES, 2).T.reshape(GRID)
    angles = np.pi * (2 * k + 1) / 256.0
    odd = 2.0 * np.arange(SPREAD) + 1.0
    weight = (2.0 / SPREAD) * np.sin(angles)
    weight = weight * np.sum(np.sin(angles[:, None] * odd) / odd, axis=1)
    columns = [np.cos(angles), np.log(np.cos(angles / 2)), np.log(np.sin(angles / 2)), weight]
    tables = [np.repeat(column[:, None], GRID, axis=1) for column in columns]
    return jnp.asarray(np.concatenate(tables, axis=0), F32)


def order_tables():
    lgamma = np.array([math.lgamma(v + 1.0) for v in range(2 * GRID + 1)])
    n = np.arange(GRID)
    p = np.where(n < SPREAD, n, n - GRID)[:, None]
    q = np.arange(SPREAD)[None, :]
    lowest = np.maximum(np.abs(p), q)
    t = np.maximum(0, q - p)
    magnitude = 0.5 * (
        lgamma[lowest + p] + lgamma[lowest - p] + lgamma[lowest + q] + lgamma[lowest - q]
    )
    magnitude = magnitude - lgamma[lowest + q - t] - lgamma[t]
    magnitude = magnitude - lgamma[p - q + t] - lgamma[lowest - p - t]
    sign = 1.0 - 2.0 * ((p - q + t) % 2)
    cos_power = 2 * lowest + q - p - 2 * t
    sin_power = p - q + 2 * t
    multiplicity = np.where(q == 0, 1.0, 2.0)
    rows = [magnitude, sign, cos_power, sin_power, lowest, p, q, multiplicity]
    rows = [np.broadcast_to(row, (GRID, SPREAD)).reshape(DEVICES, 1, 2 * SPREAD) for row in rows]
    return jnp.asarray(np.concatenate(rows, axis=1), F32)


def slot(offset):
    return offset[0] * 16 + offset[1] * 4 + offset[2]


def tile(index):
    return pl.ds(pl.multiple_of(index * 8, 8), 8)


def body(
    samples_hbm,
    packed_hbm,
    twist_hbm,
    beta_hbm,
    order_hbm,
    coef_ref,
    shares,
    samples,
    packed,
    twist,
    beta,
    order,
    spectrum,
    received,
    wigner,
    total,
    rows_of_level,
    placed,
    load_sem,
    send_sem,
    recv_sem,
):
    me = lax.axis_index("beta")
    place = (me // 16, me // 4 % 4, me % 4)

    def target(offset):
        z, y, x = ((place[axis] + offset[axis]) % 4 for axis in range(3))
        return z * 16 + y * 4 + x

    loads = [
        pltpu.make_async_copy(packed_hbm, packed, load_sem.at[0]),
        pltpu.make_async_copy(samples_hbm.at[0], samples.at[0], load_sem.at[1]),
        pltpu.make_async_copy(twist_hbm, twist, load_sem.at[2]),
        pltpu.make_async_copy(samples_hbm.at[1], samples.at[1], load_sem.at[3]),
        pltpu.make_async_copy(beta_hbm, beta, load_sem.at[4]),
        pltpu.make_async_copy(order_hbm.at[me], order, load_sem.at[5]),
    ]
    for load in loads:
        load.start()

    barrier = pltpu.get_barrier_semaphore()
    with jax.named_scope("greet"):
        for offset in OFFSETS:
            pl.semaphore_signal(
                barrier, 1, device_id={"beta": target(offset)}, device_id_type=MESH
            )

    def product(left, right):
        return jnp.dot(left, right, preferred_element_type=F32)

    def split(values):
        high = values.astype(BF16)
        return high, (values - high.astype(F32)).astype(BF16)

    def transform(k):
        high, low = split(samples[k].reshape(FUNCTIONS * GRID, GRID))
        halfway = product(jnp.concatenate([high, low], axis=1), packed[0:256, :])
        halfway = halfway + product(high, packed[256:384, :])
        twist_cos, twist_sin = twist[0:128, :], twist[128:256, :]
        alpha_high, alpha_low = packed[384:512, :], packed[512:640, :]
        for pair in range(2):
            turned = []
            for f in (2 * pair, 2 * pair + 1):
                part = halfway[f * GRID : (f + 1) * GRID]
                re, im = part[:, :128], part[:, 128:]
                turned.append(
                    jnp.concatenate(
                        [twist_cos * re + twist_sin * im, twist_cos * im - twist_sin * re], axis=0
                    )
                )
            turned_high, turned_low = split(jnp.concatenate(turned, axis=1))
            rows = (
                product(alpha_high, turned_high)
                + product(alpha_low, turned_high)
                + product(alpha_high, turned_low)
            )
            for s in range(2):
                for f in range(2):
                    spectrum[
                        pl.ds(k * HALF + s * FUNCTIONS + 2 * pair + f, DEVICES, stride=8), :
                    ] = rows[s * DEVICES : (s + 1) * DEVICES, f * 128 : (f + 1) * 128]

    def send(k):
        for offset in OFFSETS:
            other = target(offset)
            pltpu.make_async_remote_copy(
                src_ref=spectrum.at[tile(k * DEVICES + other), :],
                dst_ref=received.at[pl.ds(k * HALF + slot(offset) * 8, 8), :],
                send_sem=send_sem.at[0],
                recv_sem=recv_sem.at[k],
                device_id={"beta": other},
                device_id_type=MESH,
            ).start()

    with jax.named_scope("load"):
        for load in loads[:3]:
            load.wait()
    with jax.named_scope("dft0"):
        transform(0)
    with jax.named_scope("barrier_wait"):
        pl.semaphore_wait(barrier, OTHERS)
    with jax.named_scope("send0"):
        send(0)
    with jax.named_scope("load1"):
        for load in loads[3:]:
            load.wait()
    with jax.named_scope("dft1"):
        transform(1)
    with jax.named_scope("send1"):
        send(1)
    for k in range(2):
        received[k * HALF : k * HALF + 8, :] = spectrum[tile(k * DEVICES + me), :]

    with jax.named_scope("coeff"):
        alpha_order, gamma_order = order[5:6, :], order[6:7, :]
        lowest = order[4:5, :]
        degree = lax.broadcasted_iota(jnp.int32, (SPREAD, 128), 0).astype(F32)
        previous = degree - 1.0
        upper = (degree * degree - alpha_order * alpha_order) * (
            degree * degree - gamma_order * gamma_order
        )
        lower = (previous * previous - alpha_order * alpha_order) * (
            previous * previous - gamma_order * gamma_order
        )
        root_upper = jnp.sqrt(jnp.maximum(upper, 1.0))
        rows_of_level[0] = degree * (2.0 * previous + 1.0) / root_upper
        rows_of_level[1] = alpha_order * gamma_order / jnp.maximum(previous * degree, 1.0)
        rows_of_level[2] = (
            degree * jnp.sqrt(jnp.maximum(lower, 0.0)) / (jnp.maximum(previous, 1.0) * root_upper)
        )
        beta[128:256, :] = (
            beta[384:512, :]
            * order[1:2, :]
            * jnp.exp(
                order[0:1, :] + order[2:3, :] * beta[128:256, :] + order[3:4, :] * beta[256:384, :]
            )
        )

        def arrange(index, _):
            z = (place[0] + 4 - index // 16) % 4
            y = (place[1] + 4 - index // 4 % 4) % 4
            x = (place[2] + 4 - index % 4) % 4
            sender = z * 16 + y * 4 + x
            for k in range(2):
                for table in range(2):
                    placed[table, pl.ds(k * DEVICES + index, 1), :] = beta[
                        pl.ds(table * GRID + k * DEVICES + sender, 1), :
                    ]
            return 0

        lax.fori_loop(0, DEVICES, arrange, 0, unroll=4)

    with jax.named_scope("wigner"):
        for k in range(2):

            def advance(level, carried):
                former, current = carried
                f_row = rows_of_level[0, pl.ds(level, 1), :]
                c_row = rows_of_level[1, pl.ds(level, 1), :]
                b_row = rows_of_level[2, pl.ds(level, 1), :]
                starts = lowest == level.astype(F32)
                cosine = placed[0, k * DEVICES : (k + 1) * DEVICES, :]
                first = placed[1, k * DEVICES : (k + 1) * DEVICES, :]
                recurred = f_row * (cosine - c_row) * current - b_row * former
                renewed = jnp.where(starts, first, recurred)
                wigner[pl.ds(pl.multiple_of(level * GRID + k * DEVICES, 64), DEVICES), :] = renewed
                return current, renewed

            empty = placed[0, 0:DEVICES, :] * 0.0
            lax.fori_loop(0, SPREAD, advance, (empty, empty))

    for k in range(2):
        with jax.named_scope(f"wait{k}"):
            pltpu.make_async_remote_copy(
                src_ref=spectrum.at[0 : OTHERS * 8, :],
                dst_ref=received.at[0 : OTHERS * 8, :],
                send_sem=send_sem.at[0],
                recv_sem=recv_sem.at[k],
                device_id={"beta": target(OFFSETS[0])},
                device_id_type=MESH,
            ).wait_recv()

        def contract(block, _):
            rows = [pl.ds(pl.multiple_of(block * 128 + t * 8, 8), 8) for t in range(16)]
            if k == 0:
                sums = tuple(rows_of_level[0, 0:8, :] * 0.0 for _ in range(16))
            else:
                sums = tuple(total[rows[t], :] for t in range(16))

            def gather(group, sums):
                sums = list(sums)
                base = group * 16
                for index in range(16):
                    values = received[pl.ds(pl.multiple_of(base * 8, 8) + k * HALF + index * 8, 8), :]
                    for t in range(16):
                        factor = wigner[
                            pl.ds(
                                block * 16 * GRID + base + (t * GRID + k * DEVICES + index),
                                8,
                                stride=0,
                            ),
                            :,
                        ]
                        sums[t] = sums[t] + values * factor
                return tuple(sums)

            sums = lax.fori_loop(0, 4, gather, sums)
            for t in range(16):
                total[rows[t], :] = sums[t]
            return 0

        with jax.named_scope(f"contract{k}"):
            lax.fori_loop(0, 4, contract, 0)

    with jax.named_scope("finish"):
        scale = 8.0 * jnp.sqrt(2.0 * degree + 1.0)
        coeffs = []
        for channel in range(CHANNELS):
            coeffs.append(total[pl.ds(channel, SPREAD, stride=CHANNELS), :] * scale)
        squares = jnp.concatenate(
            [coeffs[f] * coeffs[f] + coeffs[f + 4] * coeffs[f + 4] for f in range(FUNCTIONS)], axis=0
        )
        squares_high, squares_low = split(squares)
        multiplicity = jnp.broadcast_to(order[7:8, :], (16, 128)).astype(BF16)

        def lane_sum(values):
            return lax.dot_general(
                multiplicity, values, (((1,), (1,)), ((), ())), preferred_element_type=F32
            )

        energy = lane_sum(squares_high) + lane_sum(squares_low)
        lane = lax.broadcasted_iota(jnp.int32, (1, 128), 1)
        degrees = 2.0 * (lane % SPREAD).astype(F32) + 1.0
        inverse = 1.0 / (degrees * degrees)
        shares[me, 0:1, :] = energy[0:1, :128] * inverse
        shares[me, 1:2, :] = energy[0:1, 128:] * inverse

    with jax.named_scope("share_send"):
        for offset in OFFSETS:
            pltpu.make_async_remote_copy(
                src_ref=shares.at[me],
                dst_ref=shares.at[me],
                send_sem=send_sem.at[1],
                recv_sem=recv_sem.at[2],
                device_id={"beta": target(offset)},
                device_id_type=MESH,
            ).start()

    with jax.named_scope("store"):
        for channel in range(CHANNELS):
            coef_ref[0, channel] = coeffs[channel][:, :SPREAD]
            coef_ref[1, channel] = coeffs[channel][:, SPREAD:]

    with jax.named_scope("sent"):
        for k in range(2):
            pltpu.make_async_remote_copy(
                src_ref=spectrum.at[0 : OTHERS * 8, :],
                dst_ref=received.at[0 : OTHERS * 8, :],
                send_sem=send_sem.at[0],
                recv_sem=recv_sem.at[0],
                device_id={"beta": target(OFFSETS[0])},
                device_id_type=MESH,
            ).wait_send()

    with jax.named_scope("share_wait"):
        shared = pltpu.make_async_remote_copy(
            src_ref=shares.at[0:OTHERS],
            dst_ref=shares.at[0:OTHERS],
            send_sem=send_sem.at[1],
            recv_sem=recv_sem.at[2],
            device_id={"beta": target(OFFSETS[0])},
            device_id_type=MESH,
        )
        shared.wait_send()
        shared.wait_recv()


def tail(coef_ref, shares, coef_hbm, power_hbm, power, sem):
    store = pltpu.make_async_copy(coef_ref, coef_hbm, sem.at[0])
    store.start()
    sums = [shares[index] for index in range(4)]
    for index in range(4, DEVICES):
        sums[index % 4] = sums[index % 4] + shares[index]
    result = (sums[0] + sums[1]) + (sums[2] + sums[3])
    for f in range(FUNCTIONS):
        power[f : f + 1, :] = result[f // 2 : f // 2 + 1, f % 2 * 64 : f % 2 * 64 + 64]
    finish = pltpu.make_async_copy(power, power_hbm, sem.at[1])
    finish.start()
    store.wait()
    finish.wait()


def local(samples):
    packed, twist = fourier_tables()
    anywhere = pl.BlockSpec(memory_space=pl.ANY)
    vmem = pl.BlockSpec(memory_space=pltpu.VMEM)
    coef, shares = pl.pallas_call(
        body,
        out_shape=(
            pltpu.VMEM((2, CHANNELS, SPREAD, SPREAD), F32),
            pltpu.VMEM((DEVICES, 2, 128), F32),
        ),
        in_specs=[anywhere] * 5,
        out_specs=(vmem, vmem),
        scratch_shapes=[
            pltpu.VMEM((2, FUNCTIONS, GRID, GRID), F32),
            pltpu.VMEM((640, 256), BF16),
            pltpu.VMEM((256, 128), F32),
            pltpu.VMEM((512, 128), F32),
            pltpu.VMEM((8, 128), F32),
            pltpu.VMEM((2 * HALF, 128), F32),
            pltpu.VMEM((2 * HALF, 128), F32),
            pltpu.VMEM((SPREAD * GRID, 128), F32),
            pltpu.VMEM((SPREAD * CHANNELS, 128), F32),
            pltpu.VMEM((3, SPREAD, 128), F32),
            pltpu.VMEM((2, GRID, 128), F32),
            pltpu.SemaphoreType.DMA((6,)),
            pltpu.SemaphoreType.DMA((2,)),
            pltpu.SemaphoreType.DMA((3,)),
        ],
        compiler_params=pltpu.CompilerParams(collective_id=0, has_side_effects=True),
        name="rotation_transform",
    )(samples, packed, twist, beta_tables(), order_tables())
    coef, power = pl.pallas_call(
        tail,
        out_shape=(
            jax.ShapeDtypeStruct((2, CHANNELS, SPREAD, SPREAD), F32),
            jax.ShapeDtypeStruct((FUNCTIONS, SPREAD), F32),
        ),
        in_specs=[vmem, vmem],
        out_specs=(anywhere, anywhere),
        scratch_shapes=[pltpu.VMEM((FUNCTIONS, SPREAD), F32), pltpu.SemaphoreType.DMA((2,))],
        compiler_params=pltpu.CompilerParams(vmem_limit_bytes=4 * 1024 * 1024),
        name="store_results",
    )(coef, shares)
    return coef.reshape(2, 2, FUNCTIONS, SPREAD, SPREAD), power


def solution(mesh):
    return jax.shard_map(
        local,
        mesh=mesh,
        in_specs=(P("beta", "grp", None, None),),
        out_specs=(P("beta", None, "grp", None, None), P("grp", None)),
        check_vma=False,
    )
```

time: 29 us -> 27.2 us (0.938)
  local copies, waits for them, and re-layouts: 1.37 us -> 0 us
  Pallas kernels: 26.9 us -> 26.4 us
    unnamed x2 -> x0, local copies, waits for them, and re-layouts: 1.37 us -> none
    pallas_call x1, Pallas kernels: 26.9 us -> 25.6 us  [local(): pl.pallas_call(body, out_shape=(pltpu.VMEM((2, CHANNELS, SPREAD, SPREAD),...]
    pallas_call x0 -> x1, Pallas kernels: none -> 0.82 us  [local(): pl.pallas_call(tail, out_shape=(jax.ShapeDtypeStruct((2, CHANNELS, SPREAD...]
where the time goes in v3:
time: 27.2 us; the launch traced here: 27 us
  Pallas kernels  26.4 us (97%)
  between operations  0.64 us (2%)
    pallas_call x1, Pallas kernels, local(): pl.pallas_call(body, out_shape=(pltpu.VMEM((2, CHANNELS, SPREAD, SPREAD),...  25.6 us
    pallas_call x1, Pallas kernels, local(): pl.pallas_call(tail, out_shape=(jax.ShapeDtypeStruct((2, CHANNELS, SPREAD...  0.82 us

profile of v3, /device:TPU:0, one launch (start us, length us, event | category | flops | bytes accessed | tf_op | source)
XLA Modules:
  0.0 27.0 jit_solution(8587438213617345631)
XLA Ops:
  0.6 25.6 %rotation_transform.1 = (f32[2,8,64,64]{3,2,1,0:T(8,128)S(1)}, f32[64,2,128]{2,1,0:T(2,128)S(1)}) custom-call(f32[2,4,128,128]{3,2,1,0:T(8,128)} %samples_hbm.1, bf16[640,256]{1,0:T(8,128)(2,1)} %constant.24.packed_hbm, f32[256,128]{1,0:T(8,128)} %constant.12.clone.twist_hbm, f32[512,128]{1,0:T(8,128)} %constant.13.clone.beta_hbm, ...), custom_call_target="tpu_custom_call" | custom-call | tf_op jit(solution)/shard_map/rotation_transform/pallas_call | solution.py:410
  26.2 0.8 %store_results.1 = (f32[2,8,64,64]{3,2,1,0:T(8,128)}, f32[4,64]{1,0:T(4,128)}) custom-call(f32[2,8,64,64]{3,2,1,0:T(8,128)S(1)} %get-tuple-element.6.coef_ref, f32[64,2,128]{2,1,0:T(2,128)S(1)} %get-tuple-element.7.shares), custom_call_target="tpu_custom_call" | custom-call | tf_op jit(solution)/shard_map/store_results/pallas_call | solution.py:437

commit v4 on v3

--- a/solution.py
+++ b/solution.py
@@ -41,6 +41,7 @@
 
 
 OFFSETS = far_first()
+CHUNKS = (((0, 64),), ((0, 32), (32, 48), (48, 64)), ((0, 64),))
 
 
 def split_bf16(table):
@@ -102,8 +103,9 @@
     return jnp.asarray(np.concatenate(rows, axis=1), F32)
 
 
-def slot(offset):
-    return offset[0] * 16 + offset[1] * 4 + offset[2]
+def chunk_of(k, slot):
+    before = sum(len(chunks) for chunks in CHUNKS[:k])
+    return before + next(i for i, (_, end) in enumerate(CHUNKS[k]) if slot < end)
 
 
 def tile(index):
@@ -194,35 +196,34 @@
                     ] = rows[s * DEVICES : (s + 1) * DEVICES, f * 128 : (f + 1) * 128]
 
     def send(k):
-        for offset in OFFSETS:
+        for slot, offset in enumerate(OFFSETS):
             other = target(offset)
             pltpu.make_async_remote_copy(
                 src_ref=spectrum.at[tile(k * DEVICES + other), :],
-                dst_ref=received.at[pl.ds(k * HALF + slot(offset) * 8, 8), :],
+                dst_ref=received.at[pl.ds(k * HALF + slot * 8, 8), :],
                 send_sem=send_sem.at[0],
-                recv_sem=recv_sem.at[k],
+                recv_sem=recv_sem.at[chunk_of(k, slot)],
                 device_id={"beta": other},
                 device_id_type=MESH,
             ).start()
 
-    with jax.named_scope("load"):
+    with jax.named_scope("load0"):
         for load in loads[:3]:
             load.wait()
     with jax.named_scope("dft0"):
         transform(0)
-    with jax.named_scope("barrier_wait"):
-        pl.semaphore_wait(barrier, OTHERS)
-    with jax.named_scope("send0"):
-        send(0)
     with jax.named_scope("load1"):
         for load in loads[3:]:
             load.wait()
     with jax.named_scope("dft1"):
         transform(1)
-    with jax.named_scope("send1"):
+    with jax.named_scope("barrier_wait"):
+        pl.semaphore_wait(barrier, OTHERS)
+    with jax.named_scope("send"):
+        send(0)
         send(1)
     for k in range(2):
-        received[k * HALF : k * HALF + 8, :] = spectrum[tile(k * DEVICES + me), :]
+        received[k * HALF + OTHERS * 8 : (k + 1) * HALF, :] = spectrum[tile(k * DEVICES + me), :]
 
     with jax.named_scope("coeff"):
         alpha_order, gamma_order = order[5:6, :], order[6:7, :]
@@ -249,19 +250,14 @@
             )
         )
 
-        def arrange(index, _):
-            z = (place[0] + 4 - index // 16) % 4
-            y = (place[1] + 4 - index // 4 % 4) % 4
-            x = (place[2] + 4 - index % 4) % 4
-            sender = z * 16 + y * 4 + x
+    with jax.named_scope("arrange"):
+        for slot, offset in enumerate(OFFSETS + [(0, 0, 0)]):
+            sender = target(tuple((4 - step) % 4 for step in offset))
             for k in range(2):
                 for table in range(2):
-                    placed[table, pl.ds(k * DEVICES + index, 1), :] = beta[
-                        pl.ds(table * GRID + k * DEVICES + sender, 1), :
+                    placed[table, k * DEVICES + slot : k * DEVICES + slot + 1, :] = beta[
+                        pl.ds(sender + table * GRID + k * DEVICES, 1), :
                     ]
-            return 0
-
-        lax.fori_loop(0, DEVICES, arrange, 0, unroll=4)
 
     with jax.named_scope("wigner"):
         for k in range(2):
@@ -282,20 +278,10 @@
             empty = placed[0, 0:DEVICES, :] * 0.0
             lax.fori_loop(0, SPREAD, advance, (empty, empty))
 
-    for k in range(2):
-        with jax.named_scope(f"wait{k}"):
-            pltpu.make_async_remote_copy(
-                src_ref=spectrum.at[0 : OTHERS * 8, :],
-                dst_ref=received.at[0 : OTHERS * 8, :],
-                send_sem=send_sem.at[0],
-                recv_sem=recv_sem.at[k],
-                device_id={"beta": target(OFFSETS[0])},
-                device_id_type=MESH,
-            ).wait_recv()
-
-        def contract(block, _):
+    def contract(k, begin, end, fresh):
+        def level_block(block, _):
             rows = [pl.ds(pl.multiple_of(block * 128 + t * 8, 8), 8) for t in range(16)]
-            if k == 0:
+            if fresh:
                 sums = tuple(rows_of_level[0, 0:8, :] * 0.0 for _ in range(16))
             else:
                 sums = tuple(total[rows[t], :] for t in range(16))
@@ -304,11 +290,13 @@
                 sums = list(sums)
                 base = group * 16
                 for index in range(16):
-                    values = received[pl.ds(pl.multiple_of(base * 8, 8) + k * HALF + index * 8, 8), :]
+                    values = received[
+                        pl.ds(pl.multiple_of(base * 8, 8) + (k * DEVICES + begin + index) * 8, 8), :
+                    ]
                     for t in range(16):
                         factor = wigner[
                             pl.ds(
-                                block * 16 * GRID + base + (t * GRID + k * DEVICES + index),
+                                block * 16 * GRID + base + (t * GRID + k * DEVICES + begin + index),
                                 8,
                                 stride=0,
                             ),
@@ -317,13 +305,27 @@
                         sums[t] = sums[t] + values * factor
                 return tuple(sums)
 
-            sums = lax.fori_loop(0, 4, gather, sums)
+            sums = lax.fori_loop(0, (end - begin) // 16, gather, sums)
             for t in range(16):
                 total[rows[t], :] = sums[t]
             return 0
 
-        with jax.named_scope(f"contract{k}"):
-            lax.fori_loop(0, 4, contract, 0)
+        lax.fori_loop(0, 4, level_block, 0)
+
+    for k in range(2):
+        for begin, end in CHUNKS[k][::-1]:
+            count = min(end, OTHERS) - begin
+            with jax.named_scope(f"wait{k}_{begin}"):
+                pltpu.make_async_remote_copy(
+                    src_ref=spectrum.at[0 : count * 8, :],
+                    dst_ref=received.at[0 : count * 8, :],
+                    send_sem=send_sem.at[0],
+                    recv_sem=recv_sem.at[chunk_of(k, begin)],
+                    device_id={"beta": target(OFFSETS[0])},
+                    device_id_type=MESH,
+                ).wait_recv()
+            with jax.named_scope(f"contract{k}_{begin}"):
+                contract(k, begin, end, k == 0 and begin == 0)
 
     with jax.named_scope("finish"):
         scale = 8.0 * jnp.sqrt(2.0 * degree + 1.0)
@@ -354,7 +356,7 @@
                 src_ref=shares.at[me],
                 dst_ref=shares.at[me],
                 send_sem=send_sem.at[1],
-                recv_sem=recv_sem.at[2],
+                recv_sem=recv_sem.at[chunk_of(2, 0)],
                 device_id={"beta": target(offset)},
                 device_id_type=MESH,
             ).start()
@@ -380,7 +382,7 @@
             src_ref=shares.at[0:OTHERS],
             dst_ref=shares.at[0:OTHERS],
             send_sem=send_sem.at[1],
-            recv_sem=recv_sem.at[2],
+            recv_sem=recv_sem.at[chunk_of(2, 0)],
             device_id={"beta": target(OFFSETS[0])},
             device_id_type=MESH,
         )
@@ -429,7 +431,7 @@
             pltpu.VMEM((2, GRID, 128), F32),
             pltpu.SemaphoreType.DMA((6,)),
             pltpu.SemaphoreType.DMA((2,)),
-            pltpu.SemaphoreType.DMA((3,)),
+            pltpu.SemaphoreType.DMA((sum(map(len, CHUNKS)),)),
         ],
         compiler_params=pltpu.CompilerParams(collective_id=0, has_side_effects=True),
         name="rotation_transform",

time: 27.2 us -> 26.6 us (0.978)
  Pallas kernels: 26.4 us -> 25.8 us
    pallas_call x1, Pallas kernels: 25.6 us -> 25 us  [local(): pl.pallas_call(body, out_shape=(pltpu.VMEM((2, CHANNELS, SPREAD, SPREAD),...]
where the time goes in v4:
time: 26.6 us; the launch traced here: 26.4 us
  Pallas kernels  25.8 us (97%)
  between operations  0.64 us (2%)
    pallas_call x1, Pallas kernels, local(): pl.pallas_call(body, out_shape=(pltpu.VMEM((2, CHANNELS, SPREAD, SPREAD),...  25 us
    pallas_call x1, Pallas kernels, local(): pl.pallas_call(tail, out_shape=(jax.ShapeDtypeStruct((2, CHANNELS, SPREAD...  0.82 us

profile of v4, /device:TPU:0, one launch (start us, length us, event | category | flops | bytes accessed | tf_op | source)
XLA Modules:
  0.0 26.4 jit_solution(16132102782938215172)
XLA Ops:
  0.6 25.0 %rotation_transform.1 = (f32[2,8,64,64]{3,2,1,0:T(8,128)S(1)}, f32[64,2,128]{2,1,0:T(2,128)S(1)}) custom-call(f32[2,4,128,128]{3,2,1,0:T(8,128)} %samples_hbm.1, bf16[640,256]{1,0:T(8,128)(2,1)} %constant.24.packed_hbm, f32[256,128]{1,0:T(8,128)} %constant.12.clone.twist_hbm, f32[512,128]{1,0:T(8,128)} %constant.13.clone.beta_hbm, ...), custom_call_target="tpu_custom_call" | custom-call | tf_op jit(solution)/shard_map/rotation_transform/pallas_call | solution.py:412
  25.6 0.8 %store_results.1 = (f32[2,8,64,64]{3,2,1,0:T(8,128)}, f32[4,64]{1,0:T(4,128)}) custom-call(f32[2,8,64,64]{3,2,1,0:T(8,128)S(1)} %get-tuple-element.6.coef_ref, f32[64,2,128]{2,1,0:T(2,128)S(1)} %get-tuple-element.7.shares), custom_call_target="tpu_custom_call" | custom-call | tf_op jit(solution)/shard_map/store_results/pallas_call | solution.py:439

commit v5 on v4

--- a/solution.py
+++ b/solution.py
@@ -20,27 +20,23 @@
 DEVICES = 64
 OTHERS = DEVICES - 1
 HALF = DEVICES * CHANNELS
-RING_HOPS = (0, 1, 2, 1)
-
-
-def hops(offset):
-    return sum(RING_HOPS[step] for step in offset)
-
-
-def far_first():
-    near = sorted(
-        (o for o in itertools.product(range(4), repeat=3) if o != (0, 0, 0)), key=hops
-    )
+SEND_COST = (0.0, 1.0, 2.2, 1.65)
+GREET_COST = (0.0, 1.65, 2.2, 1.0)
+
+
+def far_first(cost):
+    near = [o for o in itertools.product(range(4), repeat=3) if o != (0, 0, 0)]
     order = []
     for z, y, x in near:
         for turn in ((z, y, x), (y, x, z), (x, z, y)):
             for offset in (turn, tuple((4 - step) % 4 for step in turn)):
                 if offset not in order:
                     order.append(offset)
-    return order[::-1]
-
-
-OFFSETS = far_first()
+    return sorted(order, key=lambda o: -sum(cost[step] for step in o))
+
+
+OFFSETS = far_first(SEND_COST)
+GREETINGS = far_first(GREET_COST)
 CHUNKS = (((0, 64),), ((0, 32), (32, 48), (48, 64)), ((0, 64),))
 
 
@@ -155,7 +151,7 @@
 
     barrier = pltpu.get_barrier_semaphore()
     with jax.named_scope("greet"):
-        for offset in OFFSETS:
+        for offset in GREETINGS:
             pl.semaphore_signal(
                 barrier, 1, device_id={"beta": target(offset)}, device_id_type=MESH
             )
@@ -221,7 +217,10 @@
         pl.semaphore_wait(barrier, OTHERS)
     with jax.named_scope("send"):
         send(0)
-        send(1)
+
+        @pl.when(lax.axis_index("grp") == 0)
+        def _():
+            send(1)
     for k in range(2):
         received[k * HALF + OTHERS * 8 : (k + 1) * HALF, :] = spectrum[tile(k * DEVICES + me), :]
 
@@ -278,13 +277,20 @@
             empty = placed[0, 0:DEVICES, :] * 0.0
             lax.fori_loop(0, SPREAD, advance, (empty, empty))
 
-    def contract(k, begin, end, fresh):
+    with jax.named_scope("send_late"):
+
+        @pl.when(lax.axis_index("grp") == 1)
+        def _():
+            send(1)
+
+    smallest = jnp.minimum(2 * me, 2 * DEVICES - 1 - 2 * me)
+    first_block = smallest // 16
+    total[...] = jnp.zeros((SPREAD * CHANNELS, 128), F32)
+
+    def contract(k, begin, end):
         def level_block(block, _):
             rows = [pl.ds(pl.multiple_of(block * 128 + t * 8, 8), 8) for t in range(16)]
-            if fresh:
-                sums = tuple(rows_of_level[0, 0:8, :] * 0.0 for _ in range(16))
-            else:
-                sums = tuple(total[rows[t], :] for t in range(16))
+            sums = tuple(total[rows[t], :] for t in range(16))
 
             def gather(group, sums):
                 sums = list(sums)
@@ -310,7 +316,7 @@
                 total[rows[t], :] = sums[t]
             return 0
 
-        lax.fori_loop(0, 4, level_block, 0)
+        lax.fori_loop(first_block, 4, level_block, 0)
 
     for k in range(2):
         for begin, end in CHUNKS[k][::-1]:
@@ -325,7 +331,7 @@
                     device_id_type=MESH,
                 ).wait_recv()
             with jax.named_scope(f"contract{k}_{begin}"):
-                contract(k, begin, end, k == 0 and begin == 0)
+                contract(k, begin, end)
 
     with jax.named_scope("finish"):
         scale = 8.0 * jnp.sqrt(2.0 * degree + 1.0)

time: 26.6 us -> 26 us (0.977)
  Pallas kernels: 25.8 us -> 25.2 us
    pallas_call x1, Pallas kernels: 25 us -> 24.4 us  [local(): pl.pallas_call(body, out_shape=(pltpu.VMEM((2, CHANNELS, SPREAD, SPREAD),...]
where the time goes in v5:
time: 26 us; the launch traced here: 25.9 us
  Pallas kernels  25.2 us (97%)
  between operations  0.64 us (2%)
    pallas_call x1, Pallas kernels, local(): pl.pallas_call(body, out_shape=(pltpu.VMEM((2, CHANNELS, SPREAD, SPREAD),...  24.4 us
    pallas_call x1, Pallas kernels, local(): pl.pallas_call(tail, out_shape=(jax.ShapeDtypeStruct((2, CHANNELS, SPREAD...  0.82 us

profile of v5, /device:TPU:0, one launch (start us, length us, event | category | flops | bytes accessed | tf_op | source)
XLA Modules:
  0.0 25.9 jit_solution(3205670646375587852)
XLA Ops:
  0.6 24.4 %rotation_transform.1 = (f32[2,8,64,64]{3,2,1,0:T(8,128)S(1)}, f32[64,2,128]{2,1,0:T(2,128)S(1)}) custom-call(f32[2,4,128,128]{3,2,1,0:T(8,128)} %samples_hbm.1, bf16[640,256]{1,0:T(8,128)(2,1)} %constant.24.packed_hbm, f32[256,128]{1,0:T(8,128)} %constant.12.clone.twist_hbm, f32[512,128]{1,0:T(8,128)} %constant.13.clone.beta_hbm, ...), custom_call_target="tpu_custom_call" | custom-call | tf_op jit(solution)/shard_map/rotation_transform/pallas_call | solution.py:418
  25.1 0.8 %store_results.1 = (f32[2,8,64,64]{3,2,1,0:T(8,128)}, f32[4,64]{1,0:T(4,128)}) custom-call(f32[2,8,64,64]{3,2,1,0:T(8,128)S(1)} %get-tuple-element.6.coef_ref, f32[64,2,128]{2,1,0:T(2,128)S(1)} %get-tuple-element.7.shares), custom_call_target="tpu_custom_call" | custom-call | tf_op jit(solution)/shard_map/store_results/pallas_call | solution.py:445

commit v6 on v5

--- a/solution.py
+++ b/solution.py
@@ -20,6 +20,8 @@
 DEVICES = 64
 OTHERS = DEVICES - 1
 HALF = DEVICES * CHANNELS
+LOW = SPREAD // 2
+PACKED = 48
 SEND_COST = (0.0, 1.0, 2.2, 1.65)
 GREET_COST = (0.0, 1.65, 2.2, 1.0)
 
@@ -37,7 +39,13 @@
 
 OFFSETS = far_first(SEND_COST)
 GREETINGS = far_first(GREET_COST)
-CHUNKS = (((0, 64),), ((0, 32), (32, 48), (48, 64)), ((0, 64),))
+CHUNKS = (((0, 16), (16, 32), (32, 64)), ((0, 16), (16, 32), (32, 48), (48, 64)), ((0, 64),))
+
+
+def lanes(even, odd):
+    return np.concatenate(
+        [even[..., :LOW], odd[..., :LOW], even[..., LOW:], odd[..., LOW:]], axis=-1
+    )
 
 
 def split_bf16(table):
@@ -51,7 +59,9 @@
     q = np.arange(SPREAD)
     gamma = 2.0 * np.pi * ((g[:, None] * q[None, :]) % GRID) / GRID
     cosine, minus_sine = np.cos(gamma), -np.sin(gamma)
-    first = np.concatenate([cosine, cosine, minus_sine, minus_sine], axis=1)
+    first = np.concatenate(
+        [lanes(cosine, cosine), lanes(minus_sine, minus_sine)], axis=1
+    )
     j = np.arange(DEVICES)
     alpha = 2.0 * np.pi * ((2 * j[:, None] * g[None, :]) % GRID) / GRID
     c, s = np.cos(alpha) / GRID, np.sin(alpha) / GRID
@@ -62,8 +72,8 @@
     packed = jnp.concatenate([first_high, first_high, first_low, *split_bf16(second)], axis=0)
     turn = 2.0 * np.pi * g / GRID
     ones = np.ones((GRID, SPREAD))
-    twist_cos = np.concatenate([ones, np.cos(turn)[:, None] * ones], axis=1)
-    twist_sin = np.concatenate([0.0 * ones, np.sin(turn)[:, None] * ones], axis=1)
+    twist_cos = lanes(ones, np.cos(turn)[:, None] * ones)
+    twist_sin = lanes(0.0 * ones, np.sin(turn)[:, None] * ones)
     return packed, jnp.asarray(np.concatenate([twist_cos, twist_sin], axis=0), F32)
 
 
@@ -95,8 +105,8 @@
     sin_power = p - q + 2 * t
     multiplicity = np.where(q == 0, 1.0, 2.0)
     rows = [magnitude, sign, cos_power, sin_power, lowest, p, q, multiplicity]
-    rows = [np.broadcast_to(row, (GRID, SPREAD)).reshape(DEVICES, 1, 2 * SPREAD) for row in rows]
-    return jnp.asarray(np.concatenate(rows, axis=1), F32)
+    rows = [np.broadcast_to(row, (GRID, SPREAD)).reshape(DEVICES, 2, SPREAD) for row in rows]
+    return jnp.asarray(np.stack([lanes(row[:, 0], row[:, 1]) for row in rows], axis=1), F32)
 
 
 def chunk_of(k, slot):
@@ -270,12 +280,31 @@
                 cosine = placed[0, k * DEVICES : (k + 1) * DEVICES, :]
                 first = placed[1, k * DEVICES : (k + 1) * DEVICES, :]
                 recurred = f_row * (cosine - c_row) * current - b_row * former
-                renewed = jnp.where(starts, first, recurred)
-                wigner[pl.ds(pl.multiple_of(level * GRID + k * DEVICES, 64), DEVICES), :] = renewed
-                return current, renewed
+                return current, jnp.where(starts, first, recurred)
+
+            def where_to(row):
+                return pl.ds(pl.multiple_of(row * GRID + k * DEVICES, 64), DEVICES)
+
+            def lower(level, carried):
+                carried = advance(level, carried)
+                wigner[where_to(level), :] = carried[1]
+                return carried
+
+            def middle(level, carried):
+                carried = advance(level, carried)
+                moved = pltpu.roll(carried[1], 64, 1)
+                wigner[where_to(level - 16), :] = wigner[where_to(level - 16), :] + moved
+                return carried
+
+            def upper(level, carried):
+                carried = advance(level, carried)
+                wigner[where_to(level - 16), :] = carried[1]
+                return carried
 
             empty = placed[0, 0:DEVICES, :] * 0.0
-            lax.fori_loop(0, SPREAD, advance, (empty, empty))
+            carried = lax.fori_loop(0, 16, lower, (empty, empty))
+            carried = lax.fori_loop(16, LOW, middle, carried)
+            lax.fori_loop(LOW, SPREAD, upper, carried)
 
     with jax.named_scope("send_late"):
 
@@ -284,11 +313,35 @@
             send(1)
 
     smallest = jnp.minimum(2 * me, 2 * DEVICES - 1 - 2 * me)
-    first_block = smallest // 16
-    total[...] = jnp.zeros((SPREAD * CHANNELS, 128), F32)
+    first_block = jnp.maximum(smallest // 16 - 1, 0)
+    total[...] = jnp.zeros((PACKED * CHANNELS, 128), F32)
+    for n in range(2):
+        for channel in range(CHANNELS):
+            coef_ref[n, channel, :LOW, :] = jnp.zeros((LOW, SPREAD), F32)
+    low_lanes = lax.broadcasted_iota(jnp.int32, (8, 128), 1) < 64
+
+    scale = 8.0 * jnp.sqrt(2.0 * degree + 1.0)
+    upper_weight = jnp.broadcast_to(order[7:8, :], (16, 128)).astype(BF16)
+    lane = lax.broadcasted_iota(jnp.int32, (1, 128), 1)
+    lower_weight = jnp.broadcast_to(jnp.where(lane % LOW == 0, 1.0, 2.0), (16, 128)).astype(BF16)
+    upper_degrees = 2.0 * (LOW + lane % LOW).astype(F32) + 1.0
+    lower_degrees = 2.0 * (lane // 64 * 16 + lane % 16).astype(F32) + 1.0
+    upper_inverse = 1.0 / (upper_degrees * upper_degrees)
+    lower_inverse = 1.0 / (lower_degrees * lower_degrees)
 
     def contract(k, begin, end):
+        def fold(index, _):
+            row = index * 8
+            values = received[pl.ds(pl.multiple_of(row, 8), 8), :]
+            received[pl.ds(pl.multiple_of(row + 2 * HALF, 8), 8), :] = jnp.where(
+                low_lanes, values, pltpu.roll(values, 64, 1)
+            )
+            return 0
+
+        lax.fori_loop(k * DEVICES + begin, k * DEVICES + end, fold, 0, unroll=8)
+
         def level_block(block, _):
+            shift = jnp.where(block == 0, 2 * HALF, 0)
             rows = [pl.ds(pl.multiple_of(block * 128 + t * 8, 8), 8) for t in range(16)]
             sums = tuple(total[rows[t], :] for t in range(16))
 
@@ -297,7 +350,10 @@
                 base = group * 16
                 for index in range(16):
                     values = received[
-                        pl.ds(pl.multiple_of(base * 8, 8) + (k * DEVICES + begin + index) * 8, 8), :
+                        pl.ds(
+                            pl.multiple_of(shift + base * 8, 8) + (k * DEVICES + begin + index) * 8, 8
+                        ),
+                        :,
                     ]
                     for t in range(16):
                         factor = wigner[
@@ -316,7 +372,7 @@
                 total[rows[t], :] = sums[t]
             return 0
 
-        lax.fori_loop(first_block, 4, level_block, 0)
+        lax.fori_loop(first_block, 3, level_block, 0)
 
     for k in range(2):
         for begin, end in CHUNKS[k][::-1]:
@@ -334,27 +390,33 @@
                 contract(k, begin, end)
 
     with jax.named_scope("finish"):
-        scale = 8.0 * jnp.sqrt(2.0 * degree + 1.0)
-        coeffs = []
+        lower_scale = jnp.where(
+            lax.broadcasted_iota(jnp.int32, (16, 128), 1) < 64, scale[0:16, :], scale[16:32, :]
+        )
+        lower, upper = [], []
         for channel in range(CHANNELS):
-            coeffs.append(total[pl.ds(channel, SPREAD, stride=CHANNELS), :] * scale)
-        squares = jnp.concatenate(
-            [coeffs[f] * coeffs[f] + coeffs[f + 4] * coeffs[f + 4] for f in range(FUNCTIONS)], axis=0
-        )
-        squares_high, squares_low = split(squares)
-        multiplicity = jnp.broadcast_to(order[7:8, :], (16, 128)).astype(BF16)
-
-        def lane_sum(values):
-            return lax.dot_general(
-                multiplicity, values, (((1,), (1,)), ((), ())), preferred_element_type=F32
+            lower.append(total[pl.ds(channel, 16, stride=CHANNELS), :] * lower_scale)
+            upper.append(total[pl.ds(16 * CHANNELS + channel, LOW, stride=CHANNELS), :] * scale[LOW:, :])
+
+        def energies(values):
+            squares = [values[f] * values[f] + values[f + 4] * values[f + 4] for f in range(FUNCTIONS)]
+            return jnp.concatenate(squares, axis=0)
+
+        def lane_sum(multiplicity, squares):
+            return sum(
+                lax.dot_general(
+                    multiplicity, part, (((1,), (1,)), ((), ())), preferred_element_type=F32
+                )
+                for part in split(squares)
             )
 
-        energy = lane_sum(squares_high) + lane_sum(squares_low)
-        lane = lax.broadcasted_iota(jnp.int32, (1, 128), 1)
-        degrees = 2.0 * (lane % SPREAD).astype(F32) + 1.0
-        inverse = 1.0 / (degrees * degrees)
-        shares[me, 0:1, :] = energy[0:1, :128] * inverse
-        shares[me, 1:2, :] = energy[0:1, 128:] * inverse
+        first_half = lax.broadcasted_iota(jnp.int32, (64, 128), 1) < 64
+        folded = energies(lower)
+        folded = jnp.concatenate(
+            [jnp.where(first_half, folded, 0.0), jnp.where(first_half, 0.0, folded)], axis=0
+        )
+        shares[me, 0:1, :] = lane_sum(upper_weight, energies(upper))[0:1] * upper_inverse
+        shares[me, 1:2, :] = lane_sum(lower_weight, folded)[0:1] * lower_inverse
 
     with jax.named_scope("share_send"):
         for offset in OFFSETS:
@@ -369,8 +431,12 @@
 
     with jax.named_scope("store"):
         for channel in range(CHANNELS):
-            coef_ref[0, channel] = coeffs[channel][:, :SPREAD]
-            coef_ref[1, channel] = coeffs[channel][:, SPREAD:]
+            for n in range(2):
+                begin, end = n * LOW, (n + 1) * LOW
+                coef_ref[n, channel, 0:16, :LOW] = lower[channel][:, begin:end]
+                coef_ref[n, channel, 16:LOW, :LOW] = lower[channel][:, 64 + begin : 64 + end]
+                coef_ref[n, channel, LOW:, :LOW] = upper[channel][:, begin:end]
+                coef_ref[n, channel, LOW:, LOW:] = upper[channel][:, 64 + begin : 64 + end]
 
     with jax.named_scope("sent"):
         for k in range(2):
@@ -404,7 +470,9 @@
         sums[index % 4] = sums[index % 4] + shares[index]
     result = (sums[0] + sums[1]) + (sums[2] + sums[3])
     for f in range(FUNCTIONS):
-        power[f : f + 1, :] = result[f // 2 : f // 2 + 1, f % 2 * 64 : f % 2 * 64 + 64]
+        power[f : f + 1, 0:16] = result[1:2, f * 16 : f * 16 + 16]
+        power[f : f + 1, 16:LOW] = result[1:2, 64 + f * 16 : 64 + f * 16 + 16]
+        power[f : f + 1, LOW:] = result[0:1, f * LOW : (f + 1) * LOW]
     finish = pltpu.make_async_copy(power, power_hbm, sem.at[1])
     finish.start()
     store.wait()
@@ -430,9 +498,9 @@
             pltpu.VMEM((512, 128), F32),
             pltpu.VMEM((8, 128), F32),
             pltpu.VMEM((2 * HALF, 128), F32),
-            pltpu.VMEM((2 * HALF, 128), F32),
-            pltpu.VMEM((SPREAD * GRID, 128), F32),
-            pltpu.VMEM((SPREAD * CHANNELS, 128), F32),
+            pltpu.VMEM((4 * HALF, 128), F32),
+            pltpu.VMEM((PACKED * GRID, 128), F32),
+            pltpu.VMEM((PACKED * CHANNELS, 128), F32),
             pltpu.VMEM((3, SPREAD, 128), F32),
             pltpu.VMEM((2, GRID, 128), F32),
             pltpu.SemaphoreType.DMA((6,)),

time: 26 us -> 26.3 us (1.012)
  the two profiles are of different devices: /device:TPU:0 before, /device:TPU:1 now
where the time goes in v6:
time: 26.3 us; the launch traced here: 26.2 us
  Pallas kernels  25.5 us (97%)
  between operations  0.64 us (2%)
    pallas_call x1, Pallas kernels, local(): pl.pallas_call(body, out_shape=(pltpu.VMEM((2, CHANNELS, SPREAD, SPREAD),...  24.7 us
    pallas_call x1, Pallas kernels, local(): pl.pallas_call(tail, out_shape=(jax.ShapeDtypeStruct((2, CHANNELS, SPREAD...  0.83 us

profile of v6, /device:TPU:1, one launch (start us, length us, event | category | flops | bytes accessed | tf_op | source)
XLA Modules:
  0.0 26.2 jit_solution(15944894755710582985)
XLA Ops:
  0.6 24.7 %rotation_transform.1 = (f32[2,8,64,64]{3,2,1,0:T(8,128)S(1)}, f32[64,2,128]{2,1,0:T(2,128)S(1)}) custom-call(f32[2,4,128,128]{3,2,1,0:T(8,128)} %samples_hbm.1, bf16[640,256]{1,0:T(8,128)(2,1)} %constant.24.packed_hbm, f32[256,128]{1,0:T(8,128)} %constant.12.clone.twist_hbm, f32[512,128]{1,0:T(8,128)} %constant.13.clone.beta_hbm, ...), custom_call_target="tpu_custom_call" | custom-call | tf_op jit(solution)/shard_map/rotation_transform/pallas_call | solution.py:486
  25.4 0.8 %store_results.1 = (f32[2,8,64,64]{3,2,1,0:T(8,128)}, f32[4,64]{1,0:T(4,128)}) custom-call(f32[2,8,64,64]{3,2,1,0:T(8,128)S(1)} %get-tuple-element.6.coef_ref, f32[64,2,128]{2,1,0:T(2,128)S(1)} %get-tuple-element.7.shares), custom_call_target="tpu_custom_call" | custom-call | tf_op jit(solution)/shard_map/store_results/pallas_call | solution.py:513

commit v7 on v5

--- a/solution.py
+++ b/solution.py
@@ -37,7 +37,7 @@
 
 OFFSETS = far_first(SEND_COST)
 GREETINGS = far_first(GREET_COST)
-CHUNKS = (((0, 64),), ((0, 32), (32, 48), (48, 64)), ((0, 64),))
+CHUNKS = (((0, 16), (16, 32), (32, 48), (48, 64)), ((0, 16), (16, 32), (32, 48), (48, 64)), ((0, 64),))
 
 
 def split_bf16(table):
@@ -284,13 +284,13 @@
             send(1)
 
     smallest = jnp.minimum(2 * me, 2 * DEVICES - 1 - 2 * me)
-    first_block = smallest // 16
-    total[...] = jnp.zeros((SPREAD * CHANNELS, 128), F32)
+    first_block = smallest // 32
+    total[...] = jnp.zeros(total.shape, F32)
 
     def contract(k, begin, end):
         def level_block(block, _):
-            rows = [pl.ds(pl.multiple_of(block * 128 + t * 8, 8), 8) for t in range(16)]
-            sums = tuple(total[rows[t], :] for t in range(16))
+            rows = [pl.ds(pl.multiple_of(block * 256 + t * 8, 8), 8) for t in range(32)]
+            sums = tuple(total[rows[t], :] for t in range(32))
 
             def gather(group, sums):
                 sums = list(sums)
@@ -299,10 +299,10 @@
                     values = received[
                         pl.ds(pl.multiple_of(base * 8, 8) + (k * DEVICES + begin + index) * 8, 8), :
                     ]
-                    for t in range(16):
+                    for t in range(32):
                         factor = wigner[
                             pl.ds(
-                                block * 16 * GRID + base + (t * GRID + k * DEVICES + begin + index),
+                                block * 32 * GRID + base + (t * GRID + k * DEVICES + begin + index),
                                 8,
                                 stride=0,
                             ),
@@ -312,11 +312,11 @@
                 return tuple(sums)
 
             sums = lax.fori_loop(0, (end - begin) // 16, gather, sums)
-            for t in range(16):
+            for t in range(32):
                 total[rows[t], :] = sums[t]
             return 0
 
-        lax.fori_loop(first_block, 4, level_block, 0)
+        lax.fori_loop(first_block, 2, level_block, 0)
 
     for k in range(2):
         for begin, end in CHUNKS[k][::-1]:
@@ -429,10 +429,10 @@
             pltpu.VMEM((256, 128), F32),
             pltpu.VMEM((512, 128), F32),
             pltpu.VMEM((8, 128), F32),
+            pltpu.VMEM((2 * HALF + 8, 128), F32),
             pltpu.VMEM((2 * HALF, 128), F32),
-            pltpu.VMEM((2 * HALF, 128), F32),
-            pltpu.VMEM((SPREAD * GRID, 128), F32),
-            pltpu.VMEM((SPREAD * CHANNELS, 128), F32),
+            pltpu.VMEM((SPREAD * GRID + 8, 128), F32),
+            pltpu.VMEM((SPREAD * CHANNELS + 8, 128), F32),
             pltpu.VMEM((3, SPREAD, 128), F32),
             pltpu.VMEM((2, GRID, 128), F32),
             pltpu.SemaphoreType.DMA((6,)),

time: 26 us -> 25.8 us (level)
  no operation moved by 1% of the time
where the time goes in v7:
time: 25.8 us; the launch traced here: 25.7 us
  Pallas kernels  25 us (97%)
  between operations  0.64 us (2%)
    pallas_call x1, Pallas kernels, local(): pl.pallas_call(body, out_shape=(pltpu.VMEM((2, CHANNELS, SPREAD, SPREAD),...  24.2 us
    pallas_call x1, Pallas kernels, local(): pl.pallas_call(tail, out_shape=(jax.ShapeDtypeStruct((2, CHANNELS, SPREAD...  0.82 us

profile of v7, /device:TPU:0, one launch (start us, length us, event | category | flops | bytes accessed | tf_op | source)
XLA Modules:
  0.0 25.7 jit_solution(8822111074884956893)
XLA Ops:
  0.6 24.2 %rotation_transform.1 = (f32[2,8,64,64]{3,2,1,0:T(8,128)S(1)}, f32[64,2,128]{2,1,0:T(2,128)S(1)}) custom-call(f32[2,4,128,128]{3,2,1,0:T(8,128)} %samples_hbm.1, bf16[640,256]{1,0:T(8,128)(2,1)} %constant.24.packed_hbm, f32[256,128]{1,0:T(8,128)} %constant.12.clone.twist_hbm, f32[512,128]{1,0:T(8,128)} %constant.13.clone.beta_hbm, ...), custom_call_target="tpu_custom_call" | custom-call | tf_op jit(solution)/shard_map/rotation_transform/pallas_call | solution.py:418
  24.8 0.8 %store_results.1 = (f32[2,8,64,64]{3,2,1,0:T(8,128)}, f32[4,64]{1,0:T(4,128)}) custom-call(f32[2,8,64,64]{3,2,1,0:T(8,128)S(1)} %get-tuple-element.6.coef_ref, f32[64,2,128]{2,1,0:T(2,128)S(1)} %get-tuple-element.7.shares), custom_call_target="tpu_custom_call" | custom-call | tf_op jit(solution)/shard_map/store_results/pallas_call | solution.py:445

commit v8 on v7

--- a/solution.py
+++ b/solution.py
@@ -146,15 +146,19 @@
         pltpu.make_async_copy(beta_hbm, beta, load_sem.at[4]),
         pltpu.make_async_copy(order_hbm.at[me], order, load_sem.at[5]),
     ]
-    for load in loads:
-        load.start()
-
     barrier = pltpu.get_barrier_semaphore()
-    with jax.named_scope("greet"):
-        for offset in GREETINGS:
+
+    def greet(offsets):
+        for offset in offsets:
             pl.semaphore_signal(
                 barrier, 1, device_id={"beta": target(offset)}, device_id_type=MESH
             )
+
+    with jax.named_scope("greet"):
+        greet(GREETINGS[:7])
+        for load in loads:
+            load.start()
+        greet(GREETINGS[7:])
 
     def product(left, right):
         return jnp.dot(left, right, preferred_element_type=F32)
@@ -341,15 +345,13 @@
         squares = jnp.concatenate(
             [coeffs[f] * coeffs[f] + coeffs[f + 4] * coeffs[f + 4] for f in range(FUNCTIONS)], axis=0
         )
-        squares_high, squares_low = split(squares)
         multiplicity = jnp.broadcast_to(order[7:8, :], (16, 128)).astype(BF16)
-
-        def lane_sum(values):
-            return lax.dot_general(
-                multiplicity, values, (((1,), (1,)), ((), ())), preferred_element_type=F32
-            )
-
-        energy = lane_sum(squares_high) + lane_sum(squares_low)
+        energy = lax.dot_general(
+            jnp.concatenate([multiplicity, multiplicity], axis=1),
+            jnp.concatenate(split(squares), axis=1),
+            (((1,), (1,)), ((), ())),
+            preferred_element_type=F32,
+        )
         lane = lax.broadcasted_iota(jnp.int32, (1, 128), 1)
         degrees = 2.0 * (lane % SPREAD).astype(F32) + 1.0
         inverse = 1.0 / (degrees * degrees)

time: 25.8 us -> 25.8 us (level)
  no operation moved by 1% of the time
where the time goes in v8:
time: 25.8 us; the launch traced here: 25.7 us
  Pallas kernels  25 us (97%)
  between operations  0.64 us (2%)
    pallas_call x1, Pallas kernels, local(): pl.pallas_call(body, out_shape=(pltpu.VMEM((2, CHANNELS, SPREAD, SPREAD),...  24.2 us
    pallas_call x1, Pallas kernels, local(): pl.pallas_call(tail, out_shape=(jax.ShapeDtypeStruct((2, CHANNELS, SPREAD...  0.82 us

profile of v8, /device:TPU:0, one launch (start us, length us, event | category | flops | bytes accessed | tf_op | source)
XLA Modules:
  0.0 25.7 jit_solution(8971880244523008485)
XLA Ops:
  0.6 24.2 %rotation_transform.1 = (f32[2,8,64,64]{3,2,1,0:T(8,128)S(1)}, f32[64,2,128]{2,1,0:T(2,128)S(1)}) custom-call(f32[2,4,128,128]{3,2,1,0:T(8,128)} %samples_hbm.1, bf16[640,256]{1,0:T(8,128)(2,1)} %constant.24.packed_hbm, f32[256,128]{1,0:T(8,128)} %constant.12.clone.twist_hbm, f32[512,128]{1,0:T(8,128)} %constant.13.clone.beta_hbm, ...), custom_call_target="tpu_custom_call" | custom-call | tf_op jit(solution)/shard_map/rotation_transform/pallas_call | solution.py:420
  24.9 0.8 %store_results.1 = (f32[2,8,64,64]{3,2,1,0:T(8,128)}, f32[4,64]{1,0:T(4,128)}) custom-call(f32[2,8,64,64]{3,2,1,0:T(8,128)S(1)} %get-tuple-element.6.coef_ref, f32[64,2,128]{2,1,0:T(2,128)S(1)} %get-tuple-element.7.shares), custom_call_target="tpu_custom_call" | custom-call | tf_op jit(solution)/shard_map/store_results/pallas_call | solution.py:447
